TPU v7x, 128 devices: a whole 4x4x4 slice. The times are simulated.
128 devices in a mesh: pool: 128 (over z, y, x, core).
Axes of the slice: x: 4, y: 4, z: 4, core: 2. Of those that a mesh axis runs over, the one named last changes fastest.
Arguments:
- queries: bfloat16 [128, 256, 32, 128], P('pool')
- k_new: bfloat16 [128, 256, 8, 128], P('pool')
- v_new: bfloat16 [128, 256, 8, 128], P('pool')
- k_pool: bfloat16 [4096, 16, 8, 128], P('pool')
- v_pool: bfloat16 [4096, 16, 8, 128], P('pool')
- block_table: int32 [128, 256], replicated
- write_ids: int32 [128, 16], P('pool')
Outputs:
- output 1: bfloat16 [128, 256, 32, 128], P('pool')
- output 2: bfloat16 [4096, 16, 8, 128], P('pool')
- output 3: bfloat16 [4096, 16, 8, 128], P('pool')
All inputs are finite; a program needn't handle non-finite values.
Results may differ from a plain program's by a relative error of at most 0.00944931.
Values are sent between devices in bfloat16 or wider.
A program may use at most 1 GiB of HBM per device.

v0:
```python
import jax
import jax.numpy as jnp
from jax import lax
from jax.sharding import PartitionSpec as P


def chunk_attention(q_grp, k_pref, v_pref, k_chunk, v_chunk):
    chunk_len = q_grp.shape[1]
    score_scale = q_grp.shape[-1] ** -0.5
    s_pref = jnp.einsum('rcgqd,rtgd->rcgqt', q_grp, k_pref, preferred_element_type=jnp.float32) * score_scale
    s_self = jnp.einsum('rcgqd,rtgd->rcgqt', q_grp, k_chunk, preferred_element_type=jnp.float32) * score_scale
    causal = (jnp.arange(chunk_len)[:, None] >= jnp.arange(chunk_len)[None, :])[None, :, None, None, :]
    s_self = jnp.where(causal, s_self, -jnp.inf)
    row_max = jnp.maximum(jnp.max(s_pref, axis=-1), jnp.max(s_self, axis=-1))[..., None]
    e_pref = jnp.exp(s_pref - row_max)
    e_self = jnp.exp(s_self - row_max)
    prob_total = jnp.sum(e_pref, axis=-1, keepdims=True) + jnp.sum(e_self, axis=-1, keepdims=True)
    p_pref = (e_pref / prob_total).astype(jnp.bfloat16)
    p_self = (e_self / prob_total).astype(jnp.bfloat16)
    attn_acc = jnp.einsum('rcgqt,rtgd->rcgqd', p_pref, v_pref, preferred_element_type=jnp.float32)
    return attn_acc + jnp.einsum('rcgqt,rtgd->rcgqd', p_self, v_chunk, preferred_element_type=jnp.float32)


def solution(mesh):
    n_dev = mesh.shape['pool']

    def local_step(queries, k_new, v_new, k_pool, v_pool, block_table, write_ids):
        req_count, chunk_len, q_heads, head_dim = queries.shape
        kv_heads = k_new.shape[2]
        per_dev, block_len = k_pool.shape[0], k_pool.shape[1]
        n_pref = block_table.shape[1]
        row_cap = 2 * n_pref // n_dev + (n_pref // 2 + n_dev - 1) // n_dev
        pair_cap = req_count * row_cap
        my_index = lax.axis_index('pool')
        owners = block_table // per_dev
        owned_here = (owners == my_index).reshape(n_dev, req_count * n_pref).astype(jnp.int32)
        send_slot = jnp.where(owned_here > 0, jnp.cumsum(owned_here, axis=1) - 1, pair_cap)
        dest_dev = jnp.broadcast_to(jnp.arange(n_dev)[:, None], send_slot.shape)
        local_ids = (block_table % per_dev).reshape(n_dev, req_count * n_pref)
        send_ids = jnp.zeros((n_dev, pair_cap), jnp.int32).at[dest_dev, send_slot].set(local_ids, mode='drop')
        k_recv = lax.all_to_all(k_pool[send_ids], 'pool', 0, 0, tiled=True)
        v_recv = lax.all_to_all(v_pool[send_ids], 'pool', 0, 0, tiled=True)
        my_owners = lax.dynamic_slice_in_dim(owners, my_index * req_count, req_count, 0).reshape(-1)
        from_owner = (my_owners[:, None] == jnp.arange(n_dev)[None, :]).astype(jnp.int32)
        slot_rank = jnp.sum(from_owner * (jnp.cumsum(from_owner, axis=0) - 1), axis=1)
        recv_idx = (my_owners * pair_cap + slot_rank).reshape(req_count, n_pref)
        flat_shape = (n_dev * pair_cap, block_len, kv_heads, head_dim)
        prefix_shape = (req_count, n_pref * block_len, kv_heads, head_dim)
        k_pref = k_recv.reshape(flat_shape)[recv_idx].reshape(prefix_shape)
        v_pref = v_recv.reshape(flat_shape)[recv_idx].reshape(prefix_shape)
        q_grp = queries.reshape(req_count, chunk_len, kv_heads, q_heads // kv_heads, head_dim)
        attn_acc = chunk_attention(q_grp, k_pref, v_pref, k_new, v_new)
        attn_out = attn_acc.reshape(req_count, chunk_len, q_heads, head_dim).astype(jnp.bfloat16)
        new_shape = (req_count * chunk_len // block_len, block_len, kv_heads, head_dim)
        targets = write_ids.reshape(-1)
        k_pool_out = k_pool.at[targets].set(k_new.reshape(new_shape))
        v_pool_out = v_pool.at[targets].set(v_new.reshape(new_shape))
        return attn_out, k_pool_out, v_pool_out

    row_spec = P('pool')
    return jax.shard_map(local_step, mesh=mesh, in_specs=(row_spec, row_spec, row_spec, row_spec, row_spec, P(), row_spec), out_specs=(row_spec, row_spec, row_spec), check_vma=False)
```

profile of v0, /device:TPU:46, one launch (start us, length us, event | category | flops | bytes accessed | tf_op | source)
XLA Modules:
  0.0 954.6 jit_solution(85636760895804544)
XLA Ops:
  0.6 2.5 copy.105
  3.1 1.2 copy.104
  4.3 1.0 copy.37
  5.5 0.7 copy.75
  6.3 0.1 fusion.27
  6.6 0.8 and_reduce_fusion
  7.4 0.8 multiply_reduce_fusion
  8.4 120.3 %scatter_custom_fusion.2 = s32[640]{0:T(1024)S(1)} fusion(s32[32768]{0:T(1024)S(1)} %bitcast.114, s32[32768]{0:T(1024)} %bitcast.113, s32[]{:T(128)} %constant.28.clone.1), kind=kCustom, calls=%fused_computation.68 | custom fusion | bytes 3072
  128.8 0.2 reshape.220
  129.0 16.8 %gather_fusion = bf16[640,16,8,128]{3,2,1,0:T(8,128)(2,1)} fusion(bf16[32,16,8,128]{3,2,1,0:T(8,128)(2,1)} %copy.105, s32[1024]{0:T(1024)S(1)} %pad_clamp_fusion.1), kind=kCustom, calls=%fused_computation | custom fusion | bytes 41945600 | tf_op jit(solution)/shard_map/gather | solution.py:42
  145.8 11.5 %all-to-all-start = ((bf16[128,5,16,8,128]{4,3,2,1,0:T(8,128)(2,1)}), bf16[128,5,16,8,128]{4,3,2,1,0:T(8,128)(2,1)}, u32[]{:S(2)}, u32[]{:S(2)}) async-start(bf16[128,5,16,8,128]{4,3,2,1,0:T(8,128)(2,1)} %bitcast.102), calls=%async_computation | async-start | bytes 41943040 | tf_op jit(solution)/shard_map/all_to_all | solution.py:42
  157.4 15.6 %gather_fusion.2 = bf16[640,16,8,128]{3,2,1,0:T(8,128)(2,1)} fusion(bf16[32,16,8,128]{3,2,1,0:T(8,128)(2,1)S(1)} %copy.104, s32[1024]{0:T(1024)S(1)} %pad_clamp_fusion.1), kind=kCustom, calls=%fused_computation.2 | custom fusion | bytes 41945600 | tf_op jit(solution)/shard_map/gather | solution.py:41
  172.9 292.5 %all-to-all-done = bf16[128,5,16,8,128]{4,3,2,1,0:T(8,128)(2,1)} async-done(((bf16[128,5,16,8,128]{4,3,2,1,0:T(8,128)(2,1)}), bf16[128,5,16,8,128]{4,3,2,1,0:T(8,128)(2,1)}, u32[]{:S(2)}, u32[]{:S(2)}) %all-to-all-start) | async-done | bytes 20971552 | tf_op jit(solution)/shard_map/all_to_all | solution.py:42
  465.5 19.7 %all-to-all-start.1 = ((bf16[128,5,16,8,128]{4,3,2,1,0:T(8,128)(2,1)}), bf16[128,5,16,8,128]{4,3,2,1,0:T(8,128)(2,1)}, u32[]{:S(2)}, u32[]{:S(2)}) async-start(bf16[128,5,16,8,128]{4,3,2,1,0:T(8,128)(2,1)} %bitcast.101), calls=%async_computation.1 | async-start | bytes 41943040 | tf_op jit(solution)/shard_map/all_to_all | solution.py:41
  485.2 0.2 dynamic-slice_reduce_fusion
  485.4 0.1 copy.46
  485.5 0.2 fusion.23
  485.9 0.2 fusion.26
  486.0 0.1 copy.48
  486.2 2.9 scatter_fusion.1
  489.1 2.1 scatter_fusion
  491.2 0.2 fusion.25
  491.4 6.5 fusion.9
  497.9 15.6 %gather_fusion.1 = bf16[256,16,8,128]{3,2,1,0:T(8,128)(2,1)} fusion(bf16[640,16,8,128]{3,2,1,0:T(8,128)(2,1)} %bitcast.8, s32[1024]{0:T(1024)S(1)} %pad_clamp_fusion), kind=kCustom, calls=%fused_computation.1 | custom fusion | bytes 16778240 | tf_op jit(solution)/shard_map/gather | solution.py:50
  513.5 270.8 %all-to-all-done.1 = bf16[128,5,16,8,128]{4,3,2,1,0:T(8,128)(2,1)} async-done(((bf16[128,5,16,8,128]{4,3,2,1,0:T(8,128)(2,1)}), bf16[128,5,16,8,128]{4,3,2,1,0:T(8,128)(2,1)}, u32[]{:S(2)}, u32[]{:S(2)}) %all-to-all-start.1) | async-done | bytes 20971552 | tf_op jit(solution)/shard_map/all_to_all | solution.py:41
  784.3 15.6 %gather_fusion.3 = bf16[256,16,8,128]{3,2,1,0:T(8,128)(2,1)} fusion(bf16[640,16,8,128]{3,2,1,0:T(8,128)(2,1)} %bitcast.16, s32[1024]{0:T(1024)S(1)} %pad_clamp_fusion), kind=kCustom, calls=%fused_computation.3 | custom fusion | bytes 16778240 | tf_op jit(solution)/shard_map/gather | solution.py:49
  799.9 46.9 %bitcast_reduce_fusion = (f32[256,8,4]{0,2,1:T(4,128)S(1)}, f32[8,4096,256,4]{2,1,3,0:T(8,128)}) fusion(bf16[256,8,4,128]{3,2,1,0:T(4,128)(2,1)S(1)} %bitcast.99, bf16[4096,8,128,1]{2,1,0,3:T(8,128)(2,1)} %bitcast.103), kind=kOutput, calls=%fused_computation.8 | convolution fusion | flops 8657035264 | bytes 144736256 | tf_op jit(solution)/shard_map/rcgqd,rtgd->rcgqt/dot_general | solution.py:10
  846.8 5.1 fusion.8
  852.0 41.0 %fusion.1 = f32[256,8,4]{0,2,1:T(4,128)S(1)} fusion(f32[8,4096,256,4]{2,1,3,0:T(8,128)} %get-tuple-element.15, f32[256,8,4]{0,2,1:T(4,128)S(1)} %max.9), kind=kLoop, calls=%fused_computation.11 | loop fusion | flops 100655104 | bytes 134283264 | tf_op jit(solution)/shard_map/reduce_sum | solution.py:17
  893.0 7.6 fusion.11
  900.6 49.5 %fusion.10 = bf16[8,128,256,4]{2,1,3,0:T(8,128)(2,1)} fusion(f32[8,256,4,128]{1,3,2,0:T(8,128)} %fusion.11, f32[256,8,4]{0,2,1:T(4,128)S(1)} %add.66, f32[256,8,4]{0,2,1:T(4,128)S(1)} %max.9, f32[8,4096,256,4]{2,1,3,0:T(8,128)} %get-tuple-element.15, bf16[4096,8,128,1]{2,1,0,3:T(8,128)(2,1)} %bitcast.104), kind=kOutput, calls=%fused_computation.24 | convolution fusion | flops 8726249472 | bytes 148963328 | tf_op jit(solution)/shard_map/rcgqt,rtgd->rcgqd/dot_general | solution.py:20
  950.1 4.5 copy.58
  (36 shorter events, 0.9 us)
Async XLA Ops:
  0.6 490.8 %copy-start = (bf16[1,256,32,128]{3,2,1,0:T(8,128)(2,1)S(1)}, bf16[1,256,32,128]{3,2,1,0:T(8,128)(2,1)}, u32[]{:S(2)}) copy-start(bf16[1,256,32,128]{3,2,1,0:T(8,128)(2,1)} %param.7) | copy-start | bytes 6291460
  145.8 319.6 %all-to-all-start = ((bf16[128,5,16,8,128]{4,3,2,1,0:T(8,128)(2,1)}), bf16[128,5,16,8,128]{4,3,2,1,0:T(8,128)(2,1)}, u32[]{:S(2)}, u32[]{:S(2)}) async-start(bf16[128,5,16,8,128]{4,3,2,1,0:T(8,128)(2,1)} %bitcast.102), calls=%async_computation | async-start | bytes 41943040 | tf_op jit(solution)/shard_map/all_to_all | solution.py:42
  465.5 20.7 %copy-start.4 = (s32[1,16]{1,0:T(1,128)S(1)}, s32[1,16]{1,0:T(1,128)}, u32[]{:S(2)}) copy-start(s32[1,16]{1,0:T(1,128)} %param.13) | copy-start | bytes 196
  465.5 318.9 %all-to-all-start.1 = ((bf16[128,5,16,8,128]{4,3,2,1,0:T(8,128)(2,1)}), bf16[128,5,16,8,128]{4,3,2,1,0:T(8,128)(2,1)}, u32[]{:S(2)}, u32[]{:S(2)}) async-start(bf16[128,5,16,8,128]{4,3,2,1,0:T(8,128)(2,1)} %bitcast.101), calls=%async_computation.1 | async-start | bytes 41943040 | tf_op jit(solution)/shard_map/all_to_all | solution.py:41
  491.2 22.3 %copy-start.2 = (bf16[32,16,8,128]{3,2,1,0:T(8,128)(2,1)}, bf16[32,16,8,128]{3,2,1,0:T(8,128)(2,1)S(1)}, u32[]{:S(2)}) copy-start(bf16[32,16,8,128]{3,2,1,0:T(8,128)(2,1)S(1)} %scatter_fusion) | copy-start | bytes 3145732
  851.9 41.0 %copy-start.3 = (bf16[1,256,8,128]{3,2,1,0:T(8,128)(2,1)S(1)}, bf16[1,256,8,128]{3,2,1,0:T(8,128)(2,1)}, u32[]{:S(2)}) copy-start(bf16[1,256,8,128]{3,2,1,0:T(8,128)(2,1)} %param.9) | copy-start | bytes 1572868
  900.6 54.0 %copy-start.1 = (bf16[1,256,32,128]{3,2,1,0:T(8,128)(2,1)S(1)}, bf16[1,256,32,128]{3,2,1,0:T(8,128)(2,1)}, u32[]{:S(2)}) copy-start(bf16[1,256,32,128]{3,2,1,0:T(8,128)(2,1)} %param.7) | copy-start | bytes 6291460
where the time goes:
time: 973 us; the launch traced here: 955 us
  waiting for transfers between devices  563 us (58%)
  local copies, waits for them, and re-layouts  200 us (21%)
  matrix products  110 us (11%)
  other arithmetic  48.8 us (5%)
  starting transfers between devices  31.3 us (3%)
    all_to_all x1, waiting for transfers between devices, local_step(): v_recv = lax.all_to_all(v_pool[send_ids], 'pool', 0, 0, tiled=True)  293 us
    all_to_all x1, waiting for transfers between devices, local_step(): k_recv = lax.all_to_all(k_pool[send_ids], 'pool', 0, 0, tiled=True)  271 us
    unnamed x18, local copies, waits for them, and re-layouts  130 us
    dot_general x1, matrix products, chunk_attention(): jnp.einsum('rcgqt,rtgd->rcgqd', p_pref, v_pref, preferred_element_type=jn...  49.5 us
    dot_general x1, matrix products, chunk_attention(): jnp.einsum('rcgqd,rtgd->rcgqt', q_grp, k_pref, preferred_element_type=jnp...  46.9 us
    reduce_sum x1, other arithmetic, chunk_attention(): jnp.sum(e_pref, axis=-1, keepdims=True)  41 us
    all_to_all x1, starting transfers between devices, local_step(): k_recv = lax.all_to_all(k_pool[send_ids], 'pool', 0, 0, tiled=True)  19.7 us
  transfers between devices with their start and end apart: 2, of which 2 were waited for; matrix products, arithmetic and copies ran while one was open for 5% of the time, Pallas kernels for 0%

commit v1 on v0

--- a/solution.py
+++ b/solution.py
@@ -1,7 +1,63 @@
+import functools
+
 import jax
 import jax.numpy as jnp
 from jax import lax
+from jax.experimental import pallas as pl
+from jax.experimental.pallas import tpu as pltpu
 from jax.sharding import PartitionSpec as P
+
+
+def peer_of(me, offset):
+    z = ((me // 32) + (offset // 32)) % 4
+    y = ((me // 8) % 4 + (offset // 8) % 4) % 4
+    x = ((me // 2) % 4 + (offset // 2) % 4) % 4
+    c = (me % 2 + offset % 2) % 2
+    return z * 32 + y * 8 + x * 2 + c
+
+
+def exchange_kernel(n_dev, src_ref, dst_ref, send_sem, recv_sem, self_sem):
+    me = lax.axis_index('pool')
+    barrier = pltpu.get_barrier_semaphore()
+
+    def greet(i, carry):
+        pl.semaphore_signal(barrier, inc=1, device_id=(peer_of(me, i),), device_id_type=pl.DeviceIdType.MESH)
+        return carry
+
+    lax.fori_loop(1, n_dev, greet, 0)
+    pl.semaphore_wait(barrier, n_dev - 1)
+    own = pltpu.make_async_copy(src_ref.at[me], dst_ref.at[me], self_sem)
+    own.start()
+
+    def copy_to(i):
+        peer = peer_of(me, (i * 37) % n_dev)
+        return pltpu.make_async_remote_copy(
+            src_ref=src_ref.at[peer], dst_ref=dst_ref.at[me], send_sem=send_sem, recv_sem=recv_sem,
+            device_id=(peer,), device_id_type=pl.DeviceIdType.MESH)
+
+    def send(i, carry):
+        copy_to(i).start()
+        return carry
+
+    lax.fori_loop(1, n_dev, send, 0)
+    rest = pltpu.make_async_remote_copy(
+        src_ref=src_ref.at[pl.ds(0, n_dev - 1)], dst_ref=dst_ref.at[pl.ds(0, n_dev - 1)], send_sem=send_sem,
+        recv_sem=recv_sem, device_id=(peer_of(me, 1),), device_id_type=pl.DeviceIdType.MESH)
+    rest.wait_send()
+    rest.wait_recv()
+    own.wait()
+
+
+def exchange(blocks, collective_id):
+    n_dev = blocks.shape[0]
+    return pl.pallas_call(
+        functools.partial(exchange_kernel, n_dev),
+        out_shape=jax.ShapeDtypeStruct(blocks.shape, blocks.dtype),
+        in_specs=[pl.BlockSpec(memory_space=pl.ANY)],
+        out_specs=pl.BlockSpec(memory_space=pl.ANY),
+        scratch_shapes=[pltpu.SemaphoreType.DMA, pltpu.SemaphoreType.DMA, pltpu.SemaphoreType.DMA],
+        compiler_params=pltpu.CompilerParams(has_side_effects=True, collective_id=collective_id),
+        name='block_exchange')(blocks)
 
 
 def chunk_attention(q_grp, k_pref, v_pref, k_chunk, v_chunk):
@@ -38,8 +94,8 @@
         dest_dev = jnp.broadcast_to(jnp.arange(n_dev)[:, None], send_slot.shape)
         local_ids = (block_table % per_dev).reshape(n_dev, req_count * n_pref)
         send_ids = jnp.zeros((n_dev, pair_cap), jnp.int32).at[dest_dev, send_slot].set(local_ids, mode='drop')
-        k_recv = lax.all_to_all(k_pool[send_ids], 'pool', 0, 0, tiled=True)
-        v_recv = lax.all_to_all(v_pool[send_ids], 'pool', 0, 0, tiled=True)
+        k_recv = exchange(k_pool[send_ids], 0)
+        v_recv = exchange(v_pool[send_ids], 0)
         my_owners = lax.dynamic_slice_in_dim(owners, my_index * req_count, req_count, 0).reshape(-1)
         from_owner = (my_owners[:, None] == jnp.arange(n_dev)[None, :]).astype(jnp.int32)
         slot_rank = jnp.sum(from_owner * (jnp.cumsum(from_owner, axis=0) - 1), axis=1)

time: 973 us -> 1060 us (1.089); the launches traced: 955 us -> 1060 us
  Pallas kernels: 0 us -> 679 us
  waiting for transfers between devices: 563 us -> 0 us
  starting transfers between devices: 31.3 us -> 0 us
  local copies, waits for them, and re-layouts: 200 us -> 213 us
    pallas_call x0 -> x2, Pallas kernels: none -> 679 us  [exchange(): pl.pallas_call(functools.partial(exchange_kernel, n_dev), out_shape=jax.S...]
    all_to_all x2 -> x0, waiting for transfers between devices: 563 us -> none  [the longest x1 293 us: local_step(): v_recv = lax.all_to_all(v_pool[send_ids], 'pool', 0, 0, tiled=True)]
    all_to_all x2 -> x0, starting transfers between devices: 31.3 us -> none  [the longest x1 19.7 us: local_step(): k_recv = lax.all_to_all(k_pool[send_ids], 'pool', 0, 0, tiled=True)]
    gather x1 -> x2, local copies, waits for them, and re-layouts: 15.6 us -> 23.3 us  [local_step(): k_pref = k_recv.reshape(flat_shape)[recv_idx].reshape(prefix_shape)]
    unnamed x18 -> x22, local copies, waits for them, and re-layouts: 130 us -> 131 us
  transfers between devices with their start and end apart: 2 -> 0, of which waited for: 2 -> 0; matrix products, arithmetic and copies ran while one was open for 5% -> 0% of each run, Pallas kernels for 0% -> 0%
where the time goes in v1:
time: 1060 us
  Pallas kernels  679 us (64%)
  local copies, waits for them, and re-layouts  213 us (20%)
  matrix products  111 us (10%)
  other arithmetic  54.3 us (5%)
    pallas_call x2, Pallas kernels, exchange(): pl.pallas_call(functools.partial(exchange_kernel, n_dev), out_shape=jax.S...  679 us
    unnamed x22, local copies, waits for them, and re-layouts  131 us
    dot_general x1, matrix products, chunk_attention(): jnp.einsum('rcgqt,rtgd->rcgqd', p_pref, v_pref, preferred_element_type=jn...  49.5 us
    dot_general x1, matrix products, chunk_attention(): jnp.einsum('rcgqd,rtgd->rcgqt', q_grp, k_pref, preferred_element_type=jnp...  47.1 us
    reduce_sum x1, other arithmetic, chunk_attention(): jnp.sum(e_pref, axis=-1, keepdims=True)  41 us
    gather x2, local copies, waits for them, and re-layouts, local_step(): k_pref = k_recv.reshape(flat_shape)[recv_idx].reshape(prefix_shape)  23.3 us

profile of v1, /device:TPU:46, one launch (start us, length us, event | category | flops | bytes accessed | tf_op | source)
XLA Modules:
  0.0 1056.9 jit_solution(16067559799269103865)
XLA Ops:
  0.6 2.5 copy.101
  3.1 1.2 copy.100
  5.0 0.7 iota_compare_fusion
  5.6 1.0 copy.39
  6.7 0.7 add_select_fusion
  7.4 1.0 copy.46
  8.4 0.7 copy.75
  9.1 1.0 compare_convert_fusion.2
  10.3 0.8 copy.48
  11.0 1.0 fusion.22
  12.8 1.0 add_add_fusion
  14.0 0.8 copy.50
  14.8 1.1 fusion.24
  16.2 0.8 and_reduce_fusion
  17.0 0.8 multiply_reduce_fusion
  17.9 120.3 %scatter_custom_fusion.2 = s32[640]{0:T(1024)S(1)} fusion(s32[32768]{0:T(1024)S(1)} %bitcast.119, s32[32768]{0:T(1024)} %bitcast.118, s32[]{:T(128)} %constant.28.clone.1), kind=kCustom, calls=%fused_computation.67 | custom fusion | bytes 3072
  138.6 6.4 fusion.7
  145.0 17.9 %gather_fusion = bf16[640,16,8,128]{3,2,1,0:T(8,128)(2,1)} fusion(bf16[32,16,8,128]{3,2,1,0:T(8,128)(2,1)} %copy.101, s32[1024]{0:T(1024)S(1)} %pad_clamp_fusion.1), kind=kCustom, calls=%fused_computation | custom fusion | bytes 41945600 | tf_op jit(solution)/shard_map/gather | solution.py:98
  162.9 2.9 scatter_fusion.1
  165.8 309.9 %block_exchange.2 = bf16[128,5,16,8,128]{4,3,2,1,0:T(8,128)(2,1)} custom-call(bf16[128,5,16,8,128]{4,3,2,1,0:T(8,128)(2,1)} %bitcast.105), custom_call_target="tpu_custom_call" | custom-call | tf_op jit(solution)/shard_map/block_exchange/pallas_call | solution.py:53
  475.8 15.6 %gather_fusion.1 = bf16[256,16,8,128]{3,2,1,0:T(8,128)(2,1)} fusion(bf16[640,16,8,128]{3,2,1,0:T(8,128)(2,1)} %bitcast.107, s32[1024]{0:T(1024)S(1)} %pad_clamp_fusion), kind=kCustom, calls=%fused_computation.1 | custom fusion | bytes 16778240 | tf_op jit(solution)/shard_map/gather | solution.py:106
  491.4 16.5 %gather_fusion.2 = bf16[640,16,8,128]{3,2,1,0:T(8,128)(2,1)} fusion(bf16[32,16,8,128]{3,2,1,0:T(8,128)(2,1)S(1)} %copy.100, s32[1024]{0:T(1024)S(1)} %pad_clamp_fusion.1), kind=kCustom, calls=%fused_computation.2 | custom fusion | bytes 41945600 | tf_op jit(solution)/shard_map/gather | solution.py:97
  507.9 2.1 scatter_fusion
  510.0 368.7 %block_exchange.3 = bf16[128,5,16,8,128]{4,3,2,1,0:T(8,128)(2,1)} custom-call(bf16[128,5,16,8,128]{4,3,2,1,0:T(8,128)(2,1)} %bitcast.104), custom_call_target="tpu_custom_call" | custom-call | tf_op jit(solution)/shard_map/block_exchange/pallas_call | solution.py:53
  878.8 15.6 %gather_fusion.3 = bf16[256,16,8,128]{3,2,1,0:T(8,128)(2,1)} fusion(bf16[640,16,8,128]{3,2,1,0:T(8,128)(2,1)} %bitcast.106, s32[1024]{0:T(1024)S(1)} %pad_clamp_fusion), kind=kCustom, calls=%fused_computation.3 | custom fusion | bytes 16778240 | tf_op jit(solution)/shard_map/gather | solution.py:105
  894.4 7.7 copy.51
  902.1 47.1 %bitcast_reduce_fusion = (f32[256,8,4]{0,2,1:T(4,128)S(1)}, f32[8,4096,256,4]{2,1,3,0:T(8,128)}) fusion(bf16[4096,8,128,1]{2,0,3,1:T(8,128)(2,1)} %bitcast.108, bf16[256,8,4,128]{3,2,1,0:T(4,128)(2,1)S(1)} %bitcast.102), kind=kOutput, calls=%fused_computation.8 | convolution fusion | flops 8657035264 | bytes 144736256 | tf_op jit(solution)/shard_map/rcgqd,rtgd->rcgqt/dot_general | solution.py:66
  949.2 5.1 fusion.6
  954.4 41.0 %fusion.1 = f32[256,8,4]{0,2,1:T(4,128)S(1)} fusion(f32[8,4096,256,4]{2,1,3,0:T(8,128)} %get-tuple-element.15, f32[256,8,4]{0,2,1:T(4,128)S(1)} %max.9), kind=kLoop, calls=%fused_computation.11 | loop fusion | flops 100655104 | bytes 134283264 | tf_op jit(solution)/shard_map/reduce_sum | solution.py:73
  995.4 7.6 fusion.9
  1003.0 49.5 %fusion.8 = bf16[8,128,256,4]{2,1,3,0:T(8,128)(2,1)} fusion(f32[8,256,4,128]{1,3,2,0:T(8,128)} %fusion.9, f32[256,8,4]{0,2,1:T(4,128)S(1)} %add.66, f32[256,8,4]{0,2,1:T(4,128)S(1)} %max.9, f32[8,4096,256,4]{2,1,3,0:T(8,128)} %get-tuple-element.15, bf16[4096,8,128,1]{2,1,0,3:T(8,128)(2,1)} %bitcast.109), kind=kOutput, calls=%fused_computation.22 | convolution fusion | flops 8726249472 | bytes 148963328 | tf_op jit(solution)/shard_map/rcgqt,rtgd->rcgqd/dot_general | solution.py:76
  1052.4 4.5 copy.60
  (39 shorter events, 2.6 us)
Async XLA Ops:
  0.6 3.7 copy-start
  6.6 2.5 copy-start.3
  12.1 0.7 copy-start.5
  510.0 368.8 %copy-start.2 = (bf16[32,16,8,128]{3,2,1,0:T(8,128)(2,1)}, bf16[32,16,8,128]{3,2,1,0:T(8,128)(2,1)S(1)}, u32[]{:S(2)}) copy-start(bf16[32,16,8,128]{3,2,1,0:T(8,128)(2,1)S(1)} %scatter_fusion) | copy-start | bytes 3145732
  902.1 47.1 %copy-start.4 = (pred[256,256]{0,1:T(8,128)(4,1)S(1)}, pred[256,256]{0,1:T(8,128)(4,1)}, u32[]{:S(2)}) copy-start(pred[256,256]{0,1:T(8,128)(4,1)} %iota_compare_fusion) | copy-start | bytes 196612
  954.4 41.0 %copy-start.6 = (bf16[1,256,8,128]{3,2,1,0:T(8,128)(2,1)S(1)}, bf16[1,256,8,128]{3,2,1,0:T(8,128)(2,1)}, u32[]{:S(2)}) copy-start(bf16[1,256,8,128]{3,2,1,0:T(8,128)(2,1)} %param.9) | copy-start | bytes 1572868
  1003.0 54.0 %copy-start.1 = (bf16[1,256,32,128]{3,2,1,0:T(8,128)(2,1)S(1)}, bf16[1,256,32,128]{3,2,1,0:T(8,128)(2,1)}, u32[]{:S(2)}) copy-start(bf16[1,256,32,128]{3,2,1,0:T(8,128)(2,1)} %param.7) | copy-start | bytes 6291460

commit v2 on v0

v2 whole, which is shorter than its diff:
```python
import functools
import math

import jax
import jax.numpy as jnp
from jax import lax
from jax.experimental import pallas as pl
from jax.experimental.pallas import tpu as pltpu
from jax.sharding import PartitionSpec as P

COMMON = 8
GROUP = 32
MESH = pl.DeviceIdType.MESH


def chunk_attention(q_grp, k_pref, v_pref, k_chunk, v_chunk):
    chunk_len = q_grp.shape[1]
    score_scale = q_grp.shape[-1] ** -0.5
    s_pref = jnp.einsum('rcgqd,rtgd->rcgqt', q_grp, k_pref, preferred_element_type=jnp.float32) * score_scale
    s_self = jnp.einsum('rcgqd,rtgd->rcgqt', q_grp, k_chunk, preferred_element_type=jnp.float32) * score_scale
    causal = (jnp.arange(chunk_len)[:, None] >= jnp.arange(chunk_len)[None, :])[None, :, None, None, :]
    s_self = jnp.where(causal, s_self, -jnp.inf)
    row_max = jnp.maximum(jnp.max(s_pref, axis=-1), jnp.max(s_self, axis=-1))[..., None]
    e_pref = jnp.exp(s_pref - row_max)
    e_self = jnp.exp(s_self - row_max)
    prob_total = jnp.sum(e_pref, axis=-1, keepdims=True) + jnp.sum(e_self, axis=-1, keepdims=True)
    p_pref = (e_pref / prob_total).astype(jnp.bfloat16)
    p_self = (e_self / prob_total).astype(jnp.bfloat16)
    attn_acc = jnp.einsum('rcgqt,rtgd->rcgqd', p_pref, v_pref, preferred_element_type=jnp.float32)
    return attn_acc + jnp.einsum('rcgqt,rtgd->rcgqd', p_self, v_chunk, preferred_element_type=jnp.float32)


def general_attention(n_dev, queries, k_new, v_new, k_pool, v_pool, block_table):
    req_count, chunk_len, q_heads, head_dim = queries.shape
    kv_heads = k_new.shape[2]
    per_dev, block_len = k_pool.shape[0], k_pool.shape[1]
    n_pref = block_table.shape[1]
    row_cap = 2 * n_pref // n_dev + (n_pref // 2 + n_dev - 1) // n_dev
    pair_cap = req_count * row_cap
    my_index = lax.axis_index('pool')
    owners = block_table // per_dev
    owned_here = (owners == my_index).reshape(n_dev, req_count * n_pref).astype(jnp.int32)
    send_slot = jnp.where(owned_here > 0, jnp.cumsum(owned_here, axis=1) - 1, pair_cap)
    dest_dev = jnp.broadcast_to(jnp.arange(n_dev)[:, None], send_slot.shape)
    local_ids = (block_table % per_dev).reshape(n_dev, req_count * n_pref)
    send_ids = jnp.zeros((n_dev, pair_cap), jnp.int32).at[dest_dev, send_slot].set(local_ids, mode='drop')
    k_recv = lax.all_to_all(k_pool[send_ids], 'pool', 0, 0, tiled=True)
    v_recv = lax.all_to_all(v_pool[send_ids], 'pool', 0, 0, tiled=True)
    my_owners = lax.dynamic_slice_in_dim(owners, my_index * req_count, req_count, 0).reshape(-1)
    from_owner = (my_owners[:, None] == jnp.arange(n_dev)[None, :]).astype(jnp.int32)
    slot_rank = jnp.sum(from_owner * (jnp.cumsum(from_owner, axis=0) - 1), axis=1)
    recv_idx = (my_owners * pair_cap + slot_rank).reshape(req_count, n_pref)
    flat_shape = (n_dev * pair_cap, block_len, kv_heads, head_dim)
    prefix_shape = (req_count, n_pref * block_len, kv_heads, head_dim)
    k_pref = k_recv.reshape(flat_shape)[recv_idx].reshape(prefix_shape)
    v_pref = v_recv.reshape(flat_shape)[recv_idx].reshape(prefix_shape)
    q_grp = queries.reshape(req_count, chunk_len, kv_heads, q_heads // kv_heads, head_dim)
    attn_acc = chunk_attention(q_grp, k_pref, v_pref, k_new, v_new)
    return attn_acc.reshape(req_count, chunk_len, q_heads, head_dim).astype(jnp.bfloat16)


def plan_exchange(block_table, per_dev, n_dev):
    me = lax.axis_index('pool')
    n_col = n_dev // 4
    owners, locals_ = block_table // per_dev, block_table % per_dev
    owner_hot = (owners[:, :, None] == jnp.arange(n_dev)).astype(jnp.bfloat16)
    local_hot = (locals_[:, :, None] == jnp.arange(per_dev)).astype(jnp.bfloat16)
    named = jnp.einsum('ril,rio->rlo', local_hot, owner_hot, preferred_element_type=jnp.float32) > 0
    use_count = jnp.sum(named.astype(jnp.int32), axis=0)
    local_id = jnp.arange(per_dev, dtype=jnp.int32)[:, None]
    none = jnp.int32(1 << 20)
    key = jnp.where(named, (use_count * per_dev + local_id)[None], none)
    least = jnp.min(key, axis=1)
    common_use = named & (key > least[:, None, :])
    common = jnp.any(common_use, axis=0)
    earlier = (local_id > local_id.T).astype(jnp.bfloat16)
    rank = jnp.dot(earlier, common.astype(jnp.bfloat16), preferred_element_type=jnp.float32).astype(jnp.int32)
    per_owner = jnp.sum(common.astype(jnp.int32), axis=0).reshape(4, n_col)
    base = jnp.cumsum(per_owner, axis=0) - per_owner
    fits = jnp.all(least < none) & jnp.all(jnp.sum(per_owner, axis=0) <= COMMON)
    in_col = base.reshape(1, n_dev) + rank
    column = jnp.arange(n_dev, dtype=jnp.int32) % n_col
    slot = column[None, :] * COMMON + in_col
    direct_ids = lax.dynamic_index_in_dim(least, me, 1, keepdims=False) % per_dev
    my_common = lax.dynamic_index_in_dim(common, me, 1, keepdims=False)
    my_rank = lax.dynamic_index_in_dim(rank, me, 1, keepdims=False)
    steps = jnp.arange(COMMON, dtype=jnp.int32)
    own_ids = jnp.sum(jnp.where(my_common[:, None] & (my_rank[:, None] == steps), local_id, 0), axis=0)
    source = (jnp.arange(n_dev, dtype=jnp.int32) // n_col)[None, :] * COMMON + rank
    here = common & (column == me % n_col)[None, :]
    col_ids = jnp.sum(jnp.where(here[:, :, None] & (in_col[:, :, None] == steps), source[:, :, None], 0), axis=(0, 1))
    mine = (lax.dynamic_index_in_dim(named, me, 0, keepdims=False) & common).T.reshape(-1)
    place = jnp.cumsum(mine.astype(jnp.int32).reshape(n_dev, per_dev), axis=1)
    before = jnp.cumsum(place[:, -1]) - place[:, -1]
    place = (place - 1 + before[:, None]).reshape(-1)
    picks = jnp.arange(n_dev, dtype=jnp.int32)
    pick_ids = jnp.sum(jnp.where(mine[:, None] & (place[:, None] == picks), slot.T.reshape(-1, 1), 0), axis=0)
    return fits, direct_ids, own_ids, col_ids, pick_ids


def device_at(z, y, x, c):
    return z * 32 + y * 8 + x * 2 + c


def fused_kernel(direct_ref, own_ref, col_ref, pick_ref, q_ref, kn_ref, vn_ref, kv_ref, o_ref,
                 zbuf, cbuf, sbuf, wbuf, pbuf, acc_ref, m_ref, l_ref,
                 z_send, z_recv, a_send, a_recv, b_send, b_recv, c_send, c_recv, w_send, w_recv):
    n_dev, kv_heads = 128, kn_ref.shape[0]
    q_rows = q_ref.shape[1]
    heads = 4
    q_tile = q_rows // heads
    scale = math.log2(math.e) * q_ref.shape[2] ** -0.5
    me = lax.axis_index('pool')
    z, y, x, c = me // 32, (me // 8) % 4, (me // 2) % 4, me % 2
    col = me % 32

    def offset_peer(i):
        o = (i * 37) % n_dev
        return device_at((z + o // 32) % 4, (y + (o // 8) % 4) % 4, (x + (o // 2) % 4) % 4, (c + o) % 2)

    barrier = pltpu.get_barrier_semaphore()

    def greet(i, carry):
        pl.semaphore_signal(barrier, inc=1, device_id=(offset_peer(i),), device_id_type=MESH)
        return carry

    lax.fori_loop(1, n_dev, greet, 0)

    for k in range(COMMON):
        zbuf[z * COMMON + k] = kv_ref[own_ref[k]]

    def fill(i, carry):
        sbuf[i] = kv_ref[direct_ref[offset_peer(i)]]
        return carry

    lax.fori_loop(1, n_dev, fill, 0)
    wbuf[0] = kv_ref[direct_ref[me]]
    pl.semaphore_wait(barrier, n_dev - 1)

    def remote(src, dst, ssem, rsem, peer):
        return pltpu.make_async_remote_copy(src_ref=src, dst_ref=dst, send_sem=ssem, recv_sem=rsem,
                                            device_id=(peer,), device_id_type=MESH)

    z_part = zbuf.at[pl.ds(z * COMMON, COMMON)]
    for s in range(1, 4):
        remote(z_part, z_part, z_send, z_recv, device_at((z + s) % 4, y, x, c)).start()

    def send_direct(group):
        def one(i, carry):
            remote(sbuf.at[i], wbuf.at[i], w_send.at[group], w_recv.at[group], offset_peer(i)).start()
            return carry
        lax.fori_loop(max(1, group * GROUP), (group + 1) * GROUP, one, 0)

    other = device_at(z, y, x, 1 - c)

    def wait_direct(group):
        size = GROUP - 1 if group == 0 else GROUP
        part = wbuf.at[pl.ds(0, size)]
        remote(part, part, w_send.at[group], w_recv.at[group], other).wait_recv()

    def attend(keys, values, first):
        def per_head(g, carry):
            k_g, v_g = keys(g), values(g)
            for h in range(heads):
                cols = pl.ds(h * q_tile, q_tile)
                s = lax.dot_general(k_g, q_ref[g, cols, :], (((1,), (1,)), ((), ())), preferred_element_type=jnp.float32)
                if first:
                    row = lax.broadcasted_iota(jnp.int32, s.shape, 0)
                    token = lax.broadcasted_iota(jnp.int32, s.shape, 1)
                    s = jnp.where(row <= token, s, -jnp.inf)
                top = jnp.max(s, axis=0, keepdims=True)
                if not first:
                    old = m_ref[g, :, cols]
                    top = jnp.maximum(top, old)
                    fade = jnp.exp2((old - top) * scale)
                e = jnp.exp2((s - top) * scale)
                total = jnp.sum(e, axis=0, keepdims=True)
                part = lax.dot_general(v_g, e.astype(jnp.bfloat16), (((0,), (0,)), ((), ())), preferred_element_type=jnp.float32)
                m_ref[g, :, cols] = top
                if first:
                    l_ref[g, :, cols] = total
                    acc_ref[g, :, cols] = part
                else:
                    l_ref[g, :, cols] = l_ref[g, :, cols] * fade + total
                    acc_ref[g, :, cols] = acc_ref[g, :, cols] * fade + part
            return carry
        lax.fori_loop(0, kv_heads, per_head, 0)

    def attend_blocks(ref, start):
        def side(which):
            def of(g):
                rows = ref[pl.ds(start, GROUP), which, g]
                return rows.reshape(GROUP * rows.shape[1], rows.shape[2])
            return of
        attend(side(0), side(1), False)

    send_direct(0)
    attend(lambda g: kn_ref[g], lambda g: vn_ref[g], True)

    remote(zbuf.at[pl.ds(0, 3 * COMMON)], zbuf.at[pl.ds(0, 3 * COMMON)], z_send, z_recv, other).wait_recv()
    for k in range(COMMON):
        cbuf[col * COMMON + k] = zbuf[col_ref[k]]
    y_first = (c == 0).astype(jnp.int32)

    def peer_a(s):
        return device_at(z, (y + s * y_first) % 4, (x + s * (1 - y_first)) % 4, c)

    def peer_b(s):
        return device_at(z, (y + s * (1 - y_first)) % 4, (x + s * y_first) % 4, c)

    def line_column(yy, xx):
        return (yy % 4) * 8 + (xx % 4) * 2 + c

    def part_of(column):
        return cbuf.at[pl.ds(column * COMMON, COMMON)]

    own_part = part_of(col)
    for s in range(1, 4):
        remote(own_part, own_part, a_send, a_recv, peer_a(s)).start()
    remote(own_part, own_part, c_send.at[0], c_recv.at[0], other).start()
    send_direct(1)
    wait_direct(0)
    attend_blocks(wbuf, 0)
    three = cbuf.at[pl.ds(0, 3 * COMMON)]
    four = cbuf.at[pl.ds(0, 4 * COMMON)]
    remote(three, three, a_send, a_recv, other).wait_recv()
    lines = [part_of(line_column(y + i * y_first, x + i * (1 - y_first))) for i in range(4)]
    for s in range(1, 4):
        for line in lines:
            remote(line, line, b_send, b_recv.at[s - 1], peer_b(s)).start()
    for line in lines[1:]:
        remote(line, line, c_send.at[0], c_recv.at[0], other).start()
    send_direct(2)
    wait_direct(1)
    attend_blocks(wbuf, GROUP)
    send_direct(3)
    for s in range(1, 4):
        remote(four, four, b_send, b_recv.at[s - 1], other).wait_recv()
        for i in range(4):
            line = part_of(line_column(y + i * y_first - s * (1 - y_first), x + i * (1 - y_first) - s * y_first))
            remote(line, line, c_send.at[s], c_recv.at[s], other).start()
    wait_direct(2)
    attend_blocks(wbuf, 2 * GROUP)
    for s in range(4):
        remote(four, four, c_send.at[s], c_recv.at[s], other).wait_recv()

    def attend_common(group, carry):
        def pick(i, inner):
            pbuf[i] = cbuf[pick_ref[group * GROUP + i]]
            return inner
        lax.fori_loop(0, GROUP, pick, 0)
        attend_blocks(pbuf, 0)
        return carry

    lax.fori_loop(0, n_dev // GROUP, attend_common, 0)
    wait_direct(3)
    attend_blocks(wbuf, 3 * GROUP)

    def finish(g, carry):
        for h in range(heads):
            cols = pl.ds(h * q_tile, q_tile)
            out = acc_ref[g, :, cols] / l_ref[g, :, cols]
            o_ref[g, cols, :] = out.T.astype(jnp.bfloat16)
        return carry

    lax.fori_loop(0, kv_heads, finish, 0)

    remote(zbuf.at[pl.ds(0, 3 * COMMON)], zbuf.at[pl.ds(0, 3 * COMMON)], z_send, z_recv, other).wait_send()
    remote(three, three, a_send, a_recv, other).wait_send()
    twelve = cbuf.at[pl.ds(0, 12 * COMMON)]
    remote(twelve, twelve, b_send, b_recv.at[0], other).wait_send()
    for s in range(4):
        remote(four, four, c_send.at[s], c_recv.at[s], other).wait_send()
    for group in range(4):
        size = GROUP - 1 if group == 0 else GROUP
        part = wbuf.at[pl.ds(0, size)]
        remote(part, part, w_send.at[group], w_recv.at[group], other).wait_send()


def fused_attention(queries, k_new, v_new, kv, direct_ids, own_ids, col_ids, pick_ids):
    _, chunk_len, q_heads, head_dim = queries.shape
    kv_heads = k_new.shape[2]
    q_grp = queries[0].transpose(1, 0, 2).reshape(kv_heads, -1, head_dim)
    k_own, v_own = k_new[0].transpose(1, 0, 2), v_new[0].transpose(1, 0, 2)
    block = kv.shape[1:]
    bf16, f32 = jnp.bfloat16, jnp.float32
    smem, vmem = pl.BlockSpec(memory_space=pltpu.SMEM), pl.BlockSpec(memory_space=pltpu.VMEM)
    dma = pltpu.SemaphoreType.DMA
    out = pl.pallas_call(
        fused_kernel,
        out_shape=jax.ShapeDtypeStruct(q_grp.shape, bf16),
        in_specs=[smem] * 4 + [vmem] * 4,
        out_specs=vmem,
        scratch_shapes=[
            pltpu.VMEM((4 * COMMON,) + block, bf16),
            pltpu.VMEM((32 * COMMON,) + block, bf16),
            pltpu.VMEM((128,) + block, bf16),
            pltpu.VMEM((128,) + block, bf16),
            pltpu.VMEM((GROUP,) + block, bf16),
            pltpu.VMEM((kv_heads, head_dim, q_grp.shape[1]), f32),
            pltpu.VMEM((kv_heads, 1, q_grp.shape[1]), f32),
            pltpu.VMEM((kv_heads, 1, q_grp.shape[1]), f32),
            dma, dma, dma, dma, dma, dma((3,)), dma((4,)), dma((4,)), dma((4,)), dma((4,)),
        ],
        compiler_params=pltpu.CompilerParams(has_side_effects=True, collective_id=0, vmem_limit_bytes=66_000_000),
        name='fused_attention')(direct_ids, own_ids, col_ids, pick_ids, q_grp, k_own, v_own, kv)
    return out.reshape(q_heads, chunk_len, head_dim).transpose(1, 0, 2)[None]


def solution(mesh):
    n_dev = mesh.shape['pool']

    def local_step(queries, k_new, v_new, k_pool, v_pool, block_table, write_ids):
        req_count, chunk_len, q_heads, head_dim = queries.shape
        kv_heads = k_new.shape[2]
        per_dev, block_len = k_pool.shape[0], k_pool.shape[1]
        fits, direct_ids, own_ids, col_ids, pick_ids = plan_exchange(block_table, per_dev, n_dev)
        kv = jnp.stack([k_pool.transpose(0, 2, 1, 3), v_pool.transpose(0, 2, 1, 3)], axis=1)
        attn_out = lax.cond(
            fits,
            lambda: fused_attention(queries, k_new, v_new, kv, direct_ids, own_ids, col_ids, pick_ids),
            lambda: general_attention(n_dev, queries, k_new, v_new, k_pool, v_pool, block_table))
        new_shape = (req_count * chunk_len // block_len, block_len, kv_heads, head_dim)
        targets = write_ids.reshape(-1)
        k_pool_out = k_pool.at[targets].set(k_new.reshape(new_shape))
        v_pool_out = v_pool.at[targets].set(v_new.reshape(new_shape))
        return attn_out, k_pool_out, v_pool_out

    row_spec = P('pool')
    return jax.shard_map(local_step, mesh=mesh, in_specs=(row_spec, row_spec, row_spec, row_spec, row_spec, P(), row_spec), out_specs=(row_spec, row_spec, row_spec), check_vma=False)
```

time: 973 us -> 353 us (0.36)
  the two profiles are of different devices: /device:TPU:46 before, /device:TPU:113 now
where the time goes in v2:
time: 353 us; the launch traced here: 352 us
  Pallas kernels  291 us (82%)
  local copies, waits for them, and re-layouts  30.1 us (9%)
  other arithmetic  20.6 us (6%)
  matrix products  7.96 us (2%)
    pallas_call x1, Pallas kernels, fused_attention(): pl.pallas_call(fused_kernel, out_shape=jax.ShapeDtypeStruct(q_grp.shape,...  291 us
    another operation x9, local copies, waits for them, and re-layouts  8.42 us
    dot_general x1, matrix products, plan_exchange(): jnp.einsum('ril,rio->rlo', local_hot, owner_hot, preferred_element_type=j...  7.84 us

profile of v2, /device:TPU:113, one launch (start us, length us, event | category | flops | bytes accessed | tf_op | source)
XLA Modules:
  0.0 352.0 jit_solution(13424894961753872695)
XLA Ops:
  0.6 1.2 copy.231
  1.9 1.6 copy.230
  3.5 1.2 fusion.52
  6.2 0.7 eq.129
  6.9 1.0 add_select_fusion.3
  7.9 7.8 %convert_reduce_fusion = (s32[32,128]{1,0:T(8,128)S(1)}, pred[128,32,128]{2,1,0:T(8,128)(4,1)S(1)}) fusion(s32[128,256]{1,0:T(8,128)S(1)} %get-tuple-element.527, s32[128,256]{1,0:T(8,128)S(1)} %get-tuple-element.526), kind=kOutput, calls=%fused_computation.103 | convolution fusion | flops 275247104 | bytes 802816 | tf_op jit(solution)/shard_map/ril,rio->rlo/dot_general | solution.py:68
  16.3 0.7 compare_reduce_fusion
  18.4 0.7 compare_reduce_fusion.1
  20.6 0.6 add_bitcast_fusion
  21.4 0.8 reduce-window.16
  22.1 1.4 eq.132
  23.6 0.6 copy_bitcast_fusion.2
  24.2 1.6 pad_maximum_fusion
  26.9 0.6 broadcast.265
  27.5 318.8 %conditional.1 = (bf16[1,256,32,128]{3,2,1,0:T(8,128)(2,1)}) conditional(s32[]{:T(128)} %convert_element_type.58, (s32[128,256]{1,0:T(8,128)S(1)}, bf16[32,16,8,128]{3,2,1,0:T(8,128)(2,1)S(1)}, bf16[32,16,8,128]{3,2,1,0:T(8,128)(2,1)S(1)}, bf16[1,256,32,128]{3,2,1,0:T(8,128)(2,1)}, bf16[1,256,8,128]{3,2,1,0:T(8,128)(2,1)S(1)}, ...), branch_computations={%region_13.24_spmd, %region_24.25_spmd} | conditional | flops 18593110016 | bytes 719978176 | solution.py:319
  27.8 0.6 broadcast_compare_fusion
  28.4 0.9 copy.183
  29.3 1.3 fusion.1
  30.5 0.7 broadcast_add_fusion
  31.3 1.6 select_reduce_fusion.1.col_ref
  33.3 0.8 copy.182
  34.3 0.8 copy.181
  35.1 0.6 select_reduce_fusion.2.own_ref
  35.7 0.8 copy.180
  36.6 6.4 %select_reduce_fusion.pick_ref = s32[128]{0:T(128)} fusion(s32[]{:T(128)} %get-tuple-element.52, s32[4096,128]{1,0:T(8,128)} %get-tuple-element.95, s32[4096]{0:T(1024)S(1)} %add.188, s32[]{:T(128)} %get-tuple-element.84, s32[4096]{0:T(1024)S(1)} %broadcast_in_dim.127, pred[4096]{0:T(1024)(128)(4,1)S(1)} %and.138), kind=kLoop, calls=%fused_computation.7 | loop fusion | flops 2097024 | bytes 2134536 | tf_op jit(solution)/shard_map/reduce_sum | solution.py:97
  43.0 2.2 copy_bitcast_fusion
  45.2 3.7 %copy.175 = bf16[1,256,32,128]{3,1,2,0:T(8,128)(2,1)} copy(bf16[1,256,32,128]{3,2,1,0:T(8,128)(2,1)} %get-tuple-element.457) | data formatting | bytes 4194304 | tf_op jit(solution)/shard_map
  48.9 291.0 %fused_attention.1 = bf16[8,1024,128]{2,1,0:T(8,128)(2,1)} custom-call(s32[128]{0:T(128)} %get-tuple-element.520.direct_ref, s32[8]{0:T(128)} %select_reduce_fusion.2.own_ref, s32[8]{0:T(128)} %select_reduce_fusion.1.col_ref, s32[128]{0:T(128)} %select_reduce_fusion.pick_ref, bf16[8,1024,128]{2,1,0:T(8,128)(2,1)} %bitcast.159, ...), custom_call_target="tpu_custom_call" | custom-call | tf_op jit(solution)/shard_map/cond/branch_1_fun/fused_attention/pallas_call | solution.py:289
  339.9 3.3 copy.154
  343.2 3.1 copy.197
  346.3 3.0 scatter_fusion.1
  349.3 2.7 scatter_fusion
  (52 shorter events, 5.6 us)
Async XLA Ops:
  1.9 25.6 %copy-start.1 = (bf16[32,16,8,128]{3,2,1,0:T(8,128)(2,1)}, bf16[32,16,8,128]{3,2,1,0:T(8,128)(2,1)S(1)}, u32[]{:S(2)}) copy-start(bf16[32,16,8,128]{3,2,1,0:T(8,128)(2,1)S(1)} %copy.231) | copy-start | bytes 3145732
  3.5 24.0 %copy-start = (bf16[32,16,8,128]{3,2,1,0:T(8,128)(2,1)}, bf16[32,16,8,128]{3,2,1,0:T(8,128)(2,1)S(1)}, u32[]{:S(2)}) copy-start(bf16[32,16,8,128]{3,2,1,0:T(8,128)(2,1)S(1)} %copy.230) | copy-start | bytes 3145732
  15.8 11.7 %copy-start.2 = (bf16[1,256,8,128]{3,2,1,0:T(8,128)(2,1)S(1)}, bf16[1,256,8,128]{3,2,1,0:T(8,128)(2,1)}, u32[]{:S(2)}) copy-start(bf16[1,256,8,128]{3,2,1,0:T(8,128)(2,1)} %param.10) | copy-start | bytes 1572868
  15.8 11.7 %copy-start.5 = (s32[128,256]{1,0:T(8,128)S(1)}, s32[128,256]{1,0:T(8,128)}, u32[]{:S(2)}) copy-start(s32[128,256]{1,0:T(8,128)} %param.14) | copy-start | bytes 393220
  17.5 3.8 %copy-start.7 = (pred[32,128]{1,0:T(8,128)(4,1)}, pred[32,128]{1,0:T(8,128)(4,1)S(1)}, u32[]{:S(2)}) copy-start(pred[32,128]{1,0:T(8,128)(4,1)S(1)} %fusion.46) | copy-start | bytes 12292
  17.8 2.8 copy-start.9
  20.6 6.8 %copy-start.6 = (s32[32,128]{1,0:T(8,128)}, s32[32,128]{1,0:T(8,128)S(1)}, u32[]{:S(2)}) copy-start(s32[32,128]{1,0:T(8,128)S(1)} %convolution_convert_fusion) | copy-start | bytes 49156
  21.3 6.2 %copy-start.8 = (pred[32,128]{1,0:T(8,128)(4,1)S(1)}, pred[32,128]{1,0:T(8,128)(4,1)}, u32[]{:S(2)}) copy-start(pred[32,128]{1,0:T(8,128)(4,1)} %copy-done.7) | copy-start | bytes 12292
  27.5 321.8 %copy-start.3 = (bf16[1,256,8,128]{3,2,1,0:T(8,128)(2,1)S(1)}, bf16[1,256,8,128]{3,2,1,0:T(8,128)(2,1)}, u32[]{:S(2)}) copy-start(bf16[1,256,8,128]{3,2,1,0:T(8,128)(2,1)} %param.10) | copy-start | bytes 1572868

commit v3 on v2

v3 whole, which is shorter than its diff:
```python
import functools
import math

import jax
import jax.numpy as jnp
from jax import lax
from jax.experimental import pallas as pl
from jax.experimental.pallas import tpu as pltpu
from jax.sharding import PartitionSpec as P

COMMON = 8
GROUP = 32
MESH = pl.DeviceIdType.MESH


def chunk_attention(q_grp, k_pref, v_pref, k_chunk, v_chunk):
    chunk_len = q_grp.shape[1]
    score_scale = q_grp.shape[-1] ** -0.5
    s_pref = jnp.einsum('rcgqd,rtgd->rcgqt', q_grp, k_pref, preferred_element_type=jnp.float32) * score_scale
    s_self = jnp.einsum('rcgqd,rtgd->rcgqt', q_grp, k_chunk, preferred_element_type=jnp.float32) * score_scale
    causal = (jnp.arange(chunk_len)[:, None] >= jnp.arange(chunk_len)[None, :])[None, :, None, None, :]
    s_self = jnp.where(causal, s_self, -jnp.inf)
    row_max = jnp.maximum(jnp.max(s_pref, axis=-1), jnp.max(s_self, axis=-1))[..., None]
    e_pref = jnp.exp(s_pref - row_max)
    e_self = jnp.exp(s_self - row_max)
    prob_total = jnp.sum(e_pref, axis=-1, keepdims=True) + jnp.sum(e_self, axis=-1, keepdims=True)
    p_pref = (e_pref / prob_total).astype(jnp.bfloat16)
    p_self = (e_self / prob_total).astype(jnp.bfloat16)
    attn_acc = jnp.einsum('rcgqt,rtgd->rcgqd', p_pref, v_pref, preferred_element_type=jnp.float32)
    return attn_acc + jnp.einsum('rcgqt,rtgd->rcgqd', p_self, v_chunk, preferred_element_type=jnp.float32)


def general_attention(n_dev, queries, k_new, v_new, k_pool, v_pool, block_table):
    req_count, chunk_len, q_heads, head_dim = queries.shape
    kv_heads = k_new.shape[2]
    per_dev, block_len = k_pool.shape[0], k_pool.shape[1]
    n_pref = block_table.shape[1]
    row_cap = 2 * n_pref // n_dev + (n_pref // 2 + n_dev - 1) // n_dev
    pair_cap = req_count * row_cap
    my_index = lax.axis_index('pool')
    owners = block_table // per_dev
    owned_here = (owners == my_index).reshape(n_dev, req_count * n_pref).astype(jnp.int32)
    send_slot = jnp.where(owned_here > 0, jnp.cumsum(owned_here, axis=1) - 1, pair_cap)
    dest_dev = jnp.broadcast_to(jnp.arange(n_dev)[:, None], send_slot.shape)
    local_ids = (block_table % per_dev).reshape(n_dev, req_count * n_pref)
    send_ids = jnp.zeros((n_dev, pair_cap), jnp.int32).at[dest_dev, send_slot].set(local_ids, mode='drop')
    k_recv = lax.all_to_all(k_pool[send_ids], 'pool', 0, 0, tiled=True)
    v_recv = lax.all_to_all(v_pool[send_ids], 'pool', 0, 0, tiled=True)
    my_owners = lax.dynamic_slice_in_dim(owners, my_index * req_count, req_count, 0).reshape(-1)
    from_owner = (my_owners[:, None] == jnp.arange(n_dev)[None, :]).astype(jnp.int32)
    slot_rank = jnp.sum(from_owner * (jnp.cumsum(from_owner, axis=0) - 1), axis=1)
    recv_idx = (my_owners * pair_cap + slot_rank).reshape(req_count, n_pref)
    flat_shape = (n_dev * pair_cap, block_len, kv_heads, head_dim)
    prefix_shape = (req_count, n_pref * block_len, kv_heads, head_dim)
    k_pref = k_recv.reshape(flat_shape)[recv_idx].reshape(prefix_shape)
    v_pref = v_recv.reshape(flat_shape)[recv_idx].reshape(prefix_shape)
    q_grp = queries.reshape(req_count, chunk_len, kv_heads, q_heads // kv_heads, head_dim)
    attn_acc = chunk_attention(q_grp, k_pref, v_pref, k_new, v_new)
    return attn_acc.reshape(req_count, chunk_len, q_heads, head_dim).astype(jnp.bfloat16)


NT = (((1,), (1,)), ((), ()))
TN = (((0,), (0,)), ((), ()))


def plan_kernel(tab_ref, plan_ref, named_ref, least_ref):
    f32, bf16, i32 = jnp.float32, jnp.bfloat16, jnp.int32
    n_dev, n_pref = tab_ref.shape
    per_dev, n_col = 32, n_dev // 4
    me = lax.axis_index('pool')
    none = 1e6

    def iota(shape, dim):
        return lax.broadcasted_iota(i32, shape, dim)

    def ones(mask):
        return jnp.where(mask, 1.0, 0.0).astype(f32)

    def dot(a, b, dims=(((1,), (0,)), ((), ()))):
        return lax.dot_general(a.astype(bf16), b.astype(bf16), dims, preferred_element_type=f32)

    local_row = iota((per_dev, n_pref), 0)
    owner_row = iota((n_dev, n_pref), 0)
    local = iota((per_dev, n_dev), 0)
    owner = iota((per_dev, n_dev), 1)

    def count_row(r, total):
        row = tab_ref[pl.ds(r, 1), :]
        named = dot(ones(local_row == row % per_dev), ones(owner_row == row // per_dev), NT)
        named_ref[r] = named
        return total + named

    use_count = lax.fori_loop(0, n_dev, count_row, jnp.zeros((per_dev, n_dev), f32), unroll=8)
    order = use_count * per_dev + local.astype(f32)

    def split_row(r, carry):
        common, worst = carry
        named = named_ref[r] > 0
        key = jnp.where(named, order, none)
        least = jnp.min(key, axis=0, keepdims=True)
        least_ref[pl.ds(r, 1), :] = least
        common = jnp.maximum(common, ones(named & (key > least)))
        return common, jnp.maximum(worst, least)

    common, worst = lax.fori_loop(0, n_dev, split_row, (jnp.zeros((per_dev, n_dev), f32), jnp.zeros((1, n_dev), f32)), unroll=8)
    tri = ones(iota((per_dev, per_dev), 0) > iota((per_dev, per_dev), 1))
    rank = dot(tri, common)
    one_row = jnp.ones((8, per_dev), f32)
    source, target = iota((n_dev, n_dev), 0), iota((n_dev, n_dev), 1)
    per_owner = dot(one_row, common)
    same_col = source % n_col == target % n_col
    base = dot(per_owner, ones(same_col & (source < target)))[:1]
    in_all = dot(per_owner, ones(same_col))[:1]
    misfit = jnp.maximum(jnp.max(ones(worst >= none)), jnp.max(ones(in_all > COMMON)))
    in_col = base + rank
    slot = (owner % n_col * COMMON).astype(f32) + in_col
    pick_me = ones(iota((8, n_dev), 1) == me)
    direct = dot(pick_me, (least_ref[...].astype(i32) % per_dev).astype(f32), NT)[:1]
    here = owner == me
    my_common = jnp.sum(jnp.where(here, common, 0.0), axis=1, keepdims=True)
    my_rank = jnp.sum(jnp.where(here, rank, 0.0), axis=1, keepdims=True)
    lane = owner.astype(f32)
    own = jnp.sum(jnp.where((my_common > 0) & (my_rank == lane), local.astype(f32), 0.0), axis=0, keepdims=True)
    in_my_col = (common > 0) & (owner % n_col == me % n_col)
    place_in_z = (owner // n_col * COMMON).astype(f32) + rank
    lane_row = iota((1, n_dev), 1)
    col = jnp.zeros((1, n_dev), f32)
    for k in range(COMMON):
        found = jnp.sum(jnp.where(in_my_col & (in_col == k), place_in_z, 0.0))
        col = jnp.where(lane_row == k, found, col)
    mine = named_ref[me] * common
    before = dot(dot(one_row, mine), ones(source < target))[:1]
    place = jnp.where(mine > 0, dot(tri, mine) + before, -1.0).T
    slot_t = slot.T
    j_lane = target.astype(f32)
    pick = jnp.zeros((n_dev, n_dev), f32)
    for l in range(per_dev):
        pick = pick + jnp.where(place[:, l:l + 1] == j_lane, slot_t[:, l:l + 1], 0.0)
    pick = jnp.sum(pick, axis=0, keepdims=True)
    plan_ref[...] = jnp.zeros(plan_ref.shape, i32)
    for i, value in enumerate((misfit + jnp.zeros((1, n_dev), f32), direct, own, col, pick)):
        plan_ref[i:i + 1, :] = value.astype(i32)


def plan_exchange(block_table):
    n_dev = block_table.shape[0]
    vmem = pl.BlockSpec(memory_space=pltpu.VMEM)
    return pl.pallas_call(
        plan_kernel,
        out_shape=jax.ShapeDtypeStruct((8, n_dev), jnp.int32),
        in_specs=[vmem],
        out_specs=vmem,
        scratch_shapes=[pltpu.VMEM((n_dev, 32, n_dev), jnp.float32), pltpu.VMEM((n_dev, n_dev), jnp.float32)],
        name='plan_exchange')(block_table)


def store_kernel(ids_ref, kp_ref, vp_ref, kn_ref, vn_ref, ko_ref, vo_ref, kv_ref):
    def block(b, carry):
        ko_ref[b] = kp_ref[b]
        vo_ref[b] = vp_ref[b]
        kv_ref[b, 0] = jnp.swapaxes(kp_ref[b], 0, 1)
        kv_ref[b, 1] = jnp.swapaxes(vp_ref[b], 0, 1)
        return carry

    def write(i, carry):
        ko_ref[ids_ref[i]] = kn_ref[i]
        vo_ref[ids_ref[i]] = vn_ref[i]
        return carry

    lax.fori_loop(0, kp_ref.shape[0], block, 0)
    lax.fori_loop(0, kn_ref.shape[0], write, 0)


def store_chunk(k_pool, v_pool, k_new, v_new, write_ids):
    n_blocks, block_len, kv_heads, head_dim = k_pool.shape
    new_shape = (write_ids.size, block_len, kv_heads, head_dim)
    vmem = pl.BlockSpec(memory_space=pltpu.VMEM)
    return pl.pallas_call(
        store_kernel,
        out_shape=(jax.ShapeDtypeStruct(k_pool.shape, k_pool.dtype), jax.ShapeDtypeStruct(v_pool.shape, v_pool.dtype),
                   jax.ShapeDtypeStruct((n_blocks, 2, kv_heads, block_len, head_dim), k_pool.dtype)),
        in_specs=[pl.BlockSpec(memory_space=pltpu.SMEM)] + [vmem] * 4,
        out_specs=(vmem, vmem, vmem),
        name='store_chunk')(write_ids.reshape(-1), k_pool, v_pool, k_new.reshape(new_shape), v_new.reshape(new_shape))


def device_at(z, y, x, c):
    return z * 32 + y * 8 + x * 2 + c


def fused_kernel(plan_ref, q_ref, kn_ref, vn_ref, kv_ref, o_ref,
                 zbuf, cbuf, sbuf, wbuf, acc_ref, m_ref, l_ref, s0, s1, s2, s3, p0, p1, p2, p3, f0, f1, f2, f3,
                 z_send, z_recv, a_send, a_recv, b_send, b_recv, c_send, c_recv, w_send, w_recv):
    n_dev, kv_heads = 128, kn_ref.shape[0]
    heads = 4
    q_tile = q_ref.shape[1] // heads
    block_len = kv_ref.shape[3]
    scale = math.log2(math.e) * q_ref.shape[2] ** -0.5
    s_bufs, p_bufs, f_bufs = (s0, s1, s2, s3), (p0, p1, p2, p3), (f0, f1, f2, f3)
    me = lax.axis_index('pool')
    z, y, x, c = me // 32, (me // 8) % 4, (me // 2) % 4, me % 2
    col = me % 32
    other = device_at(z, y, x, 1 - c)
    sign = 1 + 2 * c

    def offset_peer(i):
        r = (i * 11) % 32
        dz = jnp.where(i < 32, 0, i % 3 + 1)
        return device_at((z + dz * sign) % 4, (y + (r // 8) * sign) % 4, (x + (r // 2) % 4 * sign) % 4, (c + r) % 2)

    barrier = pltpu.get_barrier_semaphore()

    def greet(i, carry):
        pl.semaphore_signal(barrier, inc=1, device_id=(offset_peer(i),), device_id_type=MESH)
        return carry

    lax.fori_loop(1, n_dev, greet, 0)

    for k in range(COMMON):
        zbuf[z * COMMON + k] = kv_ref[plan_ref[2, k]]

    def fill(i, carry):
        sbuf[i] = kv_ref[plan_ref[1, offset_peer(i)]]
        return carry

    def fill_group(group):
        lax.fori_loop(max(1, group * GROUP), (group + 1) * GROUP, fill, 0)

    fill_group(0)
    wbuf[0] = kv_ref[plan_ref[1, me]]
    pl.semaphore_wait(barrier, n_dev - 1)

    def remote(src, dst, ssem, rsem, peer):
        return pltpu.make_async_remote_copy(src_ref=src, dst_ref=dst, send_sem=ssem, recv_sem=rsem,
                                            device_id=(peer,), device_id_type=MESH)

    z_part = zbuf.at[pl.ds(z * COMMON, COMMON)]
    for s in range(1, 4):
        remote(z_part, z_part, z_send, z_recv, device_at((z + s) % 4, y, x, c)).start()

    def send_direct(group):
        def one(i, carry):
            remote(sbuf.at[i], wbuf.at[i], w_send.at[group], w_recv.at[group], offset_peer(i)).start()
            return carry
        lax.fori_loop(max(1, group * GROUP), (group + 1) * GROUP, one, 0)

    def direct_part(group):
        size = GROUP - 1 if group == 0 else GROUP
        part = wbuf.at[pl.ds(0, size)]
        return remote(part, part, w_send.at[group], w_recv.at[group], other)

    send_direct(0)

    row = lax.broadcasted_iota(jnp.int32, (kn_ref.shape[1], q_tile), 0)
    token = lax.broadcasted_iota(jnp.int32, (kn_ref.shape[1], q_tile), 1)

    def own_head(g, carry):
        for h in range(heads):
            cols = pl.ds(h * q_tile, q_tile)
            s = lax.dot_general(kn_ref[g], q_ref[g, cols, :], NT, preferred_element_type=jnp.float32)
            s = jnp.where(row <= token, s, -jnp.inf)
            top = jnp.max(s, axis=0, keepdims=True)
            e = jnp.exp2((s - top) * scale)
            m_ref[g, :, cols] = top
            l_ref[g, :, cols] = jnp.sum(e, axis=0, keepdims=True)
            acc_ref[g, :, cols] = lax.dot_general(vn_ref[g], e.astype(jnp.bfloat16), TN, preferred_element_type=jnp.float32)
        return carry

    lax.fori_loop(0, kv_heads, own_head, 0)
    for group in range(1, 4):
        fill_group(group)

    def attend(start):
        def rows_of(which, g):
            return wbuf[pl.ds(start, GROUP), which, g].reshape(GROUP * block_len, kv_ref.shape[4])

        def score(g, h):
            s_bufs[h][...] = lax.dot_general(rows_of(0, g), q_ref[g, pl.ds(h * q_tile, q_tile), :], NT, preferred_element_type=jnp.float32)

        def weigh(g, h):
            cols = pl.ds(h * q_tile, q_tile)
            old = m_ref[g, :, cols]
            top = jnp.maximum(old, jnp.max(s_bufs[h][...], axis=0, keepdims=True))
            fade = jnp.exp2((old - top) * scale)
            e = jnp.exp2((s_bufs[h][...] - top) * scale)
            l_ref[g, :, cols] = l_ref[g, :, cols] * fade + jnp.sum(e, axis=0, keepdims=True)
            p_bufs[h][...] = e.astype(jnp.bfloat16)
            m_ref[g, :, cols] = top
            f_bufs[h][...] = fade

        def add_values(g, h):
            cols = pl.ds(h * q_tile, q_tile)
            part = lax.dot_general(rows_of(1, g), p_bufs[h][...], TN, preferred_element_type=jnp.float32)
            acc_ref[g, :, cols] = acc_ref[g, :, cols] * f_bufs[h][...] + part

        for h in range(heads):
            score(0, h)
        p_bufs[heads - 1][...] = jnp.zeros_like(p_bufs[heads - 1])
        f_bufs[heads - 1][...] = jnp.ones_like(f_bufs[heads - 1])

        def per_group(g, carry):
            following, last = jnp.minimum(g + 1, kv_heads - 1), jnp.maximum(g - 1, 0)
            for h in range(heads):
                if h == 0:
                    add_values(last, heads - 1)
                else:
                    add_values(g, h - 1)
                weigh(g, h)
                score(following, h)
            return carry

        lax.fori_loop(0, kv_heads, per_group, 0)
        add_values(kv_heads - 1, heads - 1)

    y_first = 1 - c

    def peer_a(s):
        return device_at(z, (y + s * y_first) % 4, (x + s * (1 - y_first)) % 4, c)

    def peer_b(s):
        return device_at(z, (y + s * (1 - y_first)) % 4, (x + s * y_first) % 4, c)

    def line_column(yy, xx):
        return (yy % 4) * 8 + (xx % 4) * 2 + c

    def part_of(column):
        return cbuf.at[pl.ds(column * COMMON, COMMON)]

    own_part = part_of(col)
    three = cbuf.at[pl.ds(0, 3 * COMMON)]
    four = cbuf.at[pl.ds(0, 4 * COMMON)]
    z_three = zbuf.at[pl.ds(0, 3 * COMMON)]
    lines = [part_of(line_column(y + i * y_first, x + i * (1 - y_first))) for i in range(4)]

    remote(z_three, z_three, z_send, z_recv, other).wait_recv()
    for k in range(COMMON):
        cbuf[col * COMMON + k] = zbuf[plan_ref[3, k]]
    for s in range(1, 4):
        remote(own_part, own_part, a_send, a_recv, peer_a(s)).start()
    remote(own_part, own_part, c_send.at[0], c_recv.at[0], other).start()
    send_direct(1)
    remote(three, three, a_send, a_recv, other).wait_recv()
    for s in range(1, 4):
        for line in lines:
            remote(line, line, b_send, b_recv.at[s - 1], peer_b(s)).start()
    for line in lines[1:]:
        remote(line, line, c_send.at[0], c_recv.at[0], other).start()
    send_direct(2)
    send_direct(3)

    def step(t, carry):
        for group in range(3):
            @pl.when(t == group)
            def _(group=group):
                direct_part(group).wait_recv()

        @pl.when(t == 2)
        def _():
            for s in range(1, 4):
                remote(four, four, b_send, b_recv.at[s - 1], other).wait_recv()
                for i in range(4):
                    line = part_of(line_column(y + i * y_first - s * (1 - y_first), x + i * (1 - y_first) - s * y_first))
                    remote(line, line, c_send.at[s], c_recv.at[s], other).start()

        @pl.when(t == 3)
        def _():
            for s in range(4):
                remote(four, four, c_send.at[s], c_recv.at[s], other).wait_recv()

        @pl.when((t >= 3) & (t < 7))
        def _():
            def pick(i, inner):
                wbuf[n_dev + i] = cbuf[plan_ref[4, (t - 3) * GROUP + i]]
                return inner
            lax.fori_loop(0, GROUP, pick, 0)

        @pl.when(t == 7)
        def _():
            direct_part(3).wait_recv()

        attend(jnp.where(t < 3, t, jnp.where(t < 7, 4, 3)) * GROUP)
        return carry

    lax.fori_loop(0, 8, step, 0)

    def finish(g, carry):
        for h in range(heads):
            cols = pl.ds(h * q_tile, q_tile)
            out = acc_ref[g, :, cols] / l_ref[g, :, cols]
            o_ref[g, cols, :] = out.T.astype(jnp.bfloat16)
        return carry

    lax.fori_loop(0, kv_heads, finish, 0)
    remote(z_three, z_three, z_send, z_recv, other).wait_send()
    remote(three, three, a_send, a_recv, other).wait_send()
    twelve = cbuf.at[pl.ds(0, 12 * COMMON)]
    remote(twelve, twelve, b_send, b_recv.at[0], other).wait_send()
    for s in range(4):
        remote(four, four, c_send.at[s], c_recv.at[s], other).wait_send()
    for group in range(4):
        direct_part(group).wait_send()


def fused_attention(queries, k_new, v_new, kv, plan):
    _, chunk_len, q_heads, head_dim = queries.shape
    kv_heads = k_new.shape[2]
    q_grp = queries[0].transpose(1, 0, 2).reshape(kv_heads, -1, head_dim)
    k_own, v_own = k_new[0].transpose(1, 0, 2), v_new[0].transpose(1, 0, 2)
    block = kv.shape[1:]
    q_rows, q_tile = q_grp.shape[1], q_grp.shape[1] // 4
    keys = GROUP * block[2]
    bf16, f32 = jnp.bfloat16, jnp.float32
    smem, vmem = pl.BlockSpec(memory_space=pltpu.SMEM), pl.BlockSpec(memory_space=pltpu.VMEM)
    dma = pltpu.SemaphoreType.DMA
    out = pl.pallas_call(
        fused_kernel,
        out_shape=jax.ShapeDtypeStruct(q_grp.shape, bf16),
        in_specs=[smem] + [vmem] * 4,
        out_specs=vmem,
        scratch_shapes=[
            pltpu.VMEM((4 * COMMON,) + block, bf16),
            pltpu.VMEM((32 * COMMON,) + block, bf16),
            pltpu.VMEM((128,) + block, bf16),
            pltpu.VMEM((128 + GROUP,) + block, bf16),
            pltpu.VMEM((kv_heads, head_dim, q_rows), f32),
            pltpu.VMEM((kv_heads, 1, q_rows), f32),
            pltpu.VMEM((kv_heads, 1, q_rows), f32)]
        + [pltpu.VMEM((keys, q_tile), f32)] * 4 + [pltpu.VMEM((keys, q_tile), bf16)] * 4 + [pltpu.VMEM((1, q_tile), f32)] * 4
        + [dma, dma, dma, dma, dma, dma((3,)), dma((4,)), dma((4,)), dma((4,)), dma((4,))],
        compiler_params=pltpu.CompilerParams(has_side_effects=True, collective_id=0, vmem_limit_bytes=66_000_000),
        name='fused_attention')(plan, q_grp, k_own, v_own, kv)
    return out.reshape(q_heads, chunk_len, head_dim)


def solution(mesh):
    n_dev = mesh.shape['pool']

    def local_step(queries, k_new, v_new, k_pool, v_pool, block_table, write_ids):
        plan = plan_exchange(block_table)
        k_pool_out, v_pool_out, kv = store_chunk(k_pool, v_pool, k_new, v_new, write_ids)
        by_head = lax.cond(
            plan[0, 0] == 0,
            lambda: fused_attention(queries, k_new, v_new, kv, plan),
            lambda: general_attention(n_dev, queries, k_new, v_new, k_pool, v_pool, block_table)[0].transpose(1, 0, 2))
        return by_head.transpose(1, 0, 2)[None], k_pool_out, v_pool_out

    row_spec = P('pool')
    return jax.shard_map(local_step, mesh=mesh, in_specs=(row_spec, row_spec, row_spec, row_spec, row_spec, P(), row_spec), out_specs=(row_spec, row_spec, row_spec), check_vma=False)
```

time: 353 us -> 260 us (0.74)
  the two profiles are of different devices: /device:TPU:113 before, /device:TPU:37 now
where the time goes in v3:
time: 260 us
  Pallas kernels  245 us (94%)
  local copies, waits for them, and re-layouts  13.6 us (5%)
    pallas_call x1, Pallas kernels, fused_attention(): pl.pallas_call(fused_kernel, out_shape=jax.ShapeDtypeStruct(q_grp.shape,...  231 us
    pallas_call x1, Pallas kernels, plan_exchange(): pl.pallas_call(plan_kernel, out_shape=jax.ShapeDtypeStruct((8, n_dev), jn...  8.75 us

profile of v3, /device:TPU:37, one launch (start us, length us, event | category | flops | bytes accessed | tf_op | source)
XLA Modules:
  0.0 259.6 jit_solution(4748442717236859910)
XLA Ops:
  0.6 8.8 %plan_exchange.1 = s32[8,128]{1,0:T(8,128)} custom-call(s32[128,256]{1,0:T(8,128)} %tab_ref.1), custom_call_target="tpu_custom_call" | custom-call | tf_op jit(solution)/shard_map/plan_exchange/pallas_call | solution.py:148
  9.4 1.2 slice.15
  11.2 4.9 %store_chunk.1 = (bf16[32,16,8,128]{3,2,1,0:T(8,128)(2,1)}, bf16[32,16,8,128]{3,2,1,0:T(8,128)(2,1)}, bf16[32,2,8,16,128]{4,3,2,1,0:T(8,128)(2,1)}) custom-call(s32[16]{0:T(128)} %bitcast.143, bf16[32,16,8,128]{3,2,1,0:T(8,128)(2,1)} %kp_ref.1, bf16[32,16,8,128]{3,2,1,0:T(8,128)(2,1)} %vp_ref.1, bf16[16,16,8,128]{3,2,1,0:T(8,128)(2,1)} %bitcast.132, ...), custom_call_target="tpu_custom_call" | custom-call | tf_op jit(solution)/shard_map/store_chunk/pallas_call | solution.py:178
  16.1 240.4 %conditional.1 = (bf16[32,256,128]{1,2,0:T(8,128)(2,1)S(1)}) conditional(s32[]{:T(128)} %bitcast.46, (s32[128,256]{1,0:T(8,128)}, bf16[32,16,8,128]{3,2,1,0:T(8,128)(2,1)}, bf16[32,16,8,128]{3,2,1,0:T(8,128)(2,1)}, bf16[1,256,32,128]{3,2,1,0:T(8,128)(2,1)}, bf16[1,256,8,128]{3,2,1,0:T(8,128)(2,1)}, ...), branch_computations={%region_0.11_spmd, %region_11.12_spmd} | conditional | flops 18593110016 | bytes 726269184 | solution.py:441
  16.1 2.4 copy_bitcast_fusion
  18.5 3.8 %copy.58 = bf16[1,256,32,128]{3,1,2,0:T(8,128)(2,1)} copy(bf16[1,256,32,128]{3,2,1,0:T(8,128)(2,1)} %get-tuple-element.73) | data formatting | bytes 4194304 | tf_op jit(solution)/shard_map
  22.2 231.0 %fused_attention.1 = bf16[8,1024,128]{2,1,0:T(8,128)(2,1)} custom-call(s32[8,128]{1,0:T(8,128)} %get-tuple-element.31.plan_ref, bf16[8,1024,128]{2,1,0:T(8,128)(2,1)} %bitcast.130, bf16[8,256,128]{2,1,0:T(8,128)(2,1)} %get-tuple-element.81.kn_ref, bf16[8,256,128]{2,1,0:T(8,128)(2,1)} %get-tuple-element.80.vn_ref, ...), custom_call_target="tpu_custom_call" | custom-call | tf_op jit(solution)/shard_map/cond/branch_1_fun/fused_attention/pallas_call | solution.py:415
  253.2 3.3 %copy.40 = bf16[32,256,128]{1,2,0:T(8,128)(2,1)S(1)} copy(bf16[32,256,128]{2,1,0:T(8,128)(2,1)} %bitcast.129) | data formatting | bytes 4194304 | tf_op jit(solution)/shard_map/cond/branch_1_fun/reshape | solution.py:432
  256.5 3.1 %copy.61 = bf16[32,256,128]{2,0,1:T(8,128)(2,1)} copy(bf16[32,256,128]{1,2,0:T(8,128)(2,1)S(1)} %get-tuple-element.86) | data formatting | bytes 4194304 | tf_op jit(solution)/shard_map/cond | solution.py:441

commit v4 on v3

--- a/solution.py
+++ b/solution.py
@@ -314,71 +314,85 @@
 
     y_first = 1 - c
 
-    def peer_a(s):
-        return device_at(z, (y + s * y_first) % 4, (x + s * (1 - y_first)) % 4, c)
-
-    def peer_b(s):
-        return device_at(z, (y + s * (1 - y_first)) % 4, (x + s * y_first) % 4, c)
-
-    def line_column(yy, xx):
-        return (yy % 4) * 8 + (xx % 4) * 2 + c
-
-    def part_of(column):
-        return cbuf.at[pl.ds(column * COMMON, COMMON)]
-
-    own_part = part_of(col)
-    three = cbuf.at[pl.ds(0, 3 * COMMON)]
-    four = cbuf.at[pl.ds(0, 4 * COMMON)]
+    def line_at(first, second):
+        yy = (y + first * y_first + second * (1 - y_first)) % 4
+        xx = (x + first * (1 - y_first) + second * y_first) % 4
+        return (yy * 8 + xx * 2 + c) * COMMON
+
+    def peer_at(first, second):
+        yy = (y + first * y_first + second * (1 - y_first)) % 4
+        xx = (x + first * (1 - y_first) + second * y_first) % 4
+        return device_at(z, yy, xx, c)
+
+    next_a, prev_a, next_b, prev_b = peer_at(1, 0), peer_at(3, 0), peer_at(0, 1), peer_at(0, 3)
+    half = COMMON // 2
+
+    def share(start, size, ssem, rsem, peer):
+        part = cbuf.at[pl.ds(start, size)]
+        return remote(part, part, ssem, rsem, peer)
+
+    def arrived(blocks, ssem, rsem):
+        share(0, blocks, ssem, rsem, other).wait_recv()
+
+    def to_second(i, first):
+        start = line_at(first, 0)
+        share(start, COMMON, b_send, b_recv.at[3 * i], next_b).start()
+        share(start, COMMON, b_send, b_recv.at[3 * i + 1], prev_b).start()
+        share(start, COMMON, c_send.at[0], c_recv.at[0], other).start()
+
     z_three = zbuf.at[pl.ds(0, 3 * COMMON)]
-    lines = [part_of(line_column(y + i * y_first, x + i * (1 - y_first))) for i in range(4)]
+    order = (0, 3, 1, 2)
 
     remote(z_three, z_three, z_send, z_recv, other).wait_recv()
     for k in range(COMMON):
         cbuf[col * COMMON + k] = zbuf[plan_ref[3, k]]
-    for s in range(1, 4):
-        remote(own_part, own_part, a_send, a_recv, peer_a(s)).start()
-    remote(own_part, own_part, c_send.at[0], c_recv.at[0], other).start()
-    send_direct(1)
-    remote(three, three, a_send, a_recv, other).wait_recv()
-    for s in range(1, 4):
-        for line in lines:
-            remote(line, line, b_send, b_recv.at[s - 1], peer_b(s)).start()
-    for line in lines[1:]:
-        remote(line, line, c_send.at[0], c_recv.at[0], other).start()
-    send_direct(2)
-    send_direct(3)
+    share(line_at(0, 0), COMMON, a_send, a_recv.at[0], next_a).start()
+    share(line_at(0, 0), COMMON, a_send, a_recv.at[1], prev_a).start()
+    to_second(0, 0)
+    arrived(COMMON, a_send, a_recv.at[0])
+    share(line_at(3, 0), half, a_send, a_recv.at[2], next_a).start()
+    to_second(1, 3)
+    arrived(COMMON, a_send, a_recv.at[1])
+    share(line_at(1, 0) + half, half, a_send, a_recv.at[2], prev_a).start()
+    to_second(2, 1)
+    arrived(COMMON, a_send, a_recv.at[2])
+    to_second(3, 2)
+    for i, first in enumerate(order):
+        arrived(COMMON, b_send, b_recv.at[3 * i])
+        share(line_at(first, 3), half, b_send, b_recv.at[3 * i + 2], next_b).start()
+        share(line_at(first, 3), COMMON, c_send.at[1], c_recv.at[1], other).start()
+        arrived(COMMON, b_send, b_recv.at[3 * i + 1])
+        share(line_at(first, 1) + half, half, b_send, b_recv.at[3 * i + 2], prev_b).start()
+        share(line_at(first, 1), COMMON, c_send.at[2], c_recv.at[2], other).start()
+    for group in range(1, 4):
+        send_direct(group)
+    for i, first in enumerate(order):
+        arrived(COMMON, b_send, b_recv.at[3 * i + 2])
+        share(line_at(first, 2), COMMON, c_send.at[3], c_recv.at[3], other).start()
 
     def step(t, carry):
-        for group in range(3):
-            @pl.when(t == group)
+        @pl.when(t == 0)
+        def _():
+            direct_part(0).wait_recv()
+
+        @pl.when(t == 1)
+        def _():
+            for i in range(4):
+                arrived(4 * COMMON, c_send.at[i], c_recv.at[i])
+
+        @pl.when((t >= 1) & (t < 5))
+        def _():
+            def pick(i, inner):
+                wbuf[n_dev + i] = cbuf[plan_ref[4, (t - 1) * GROUP + i]]
+                return inner
+            lax.fori_loop(0, GROUP, pick, 0)
+
+        for group in range(1, 4):
+            @pl.when(t == group + 4)
             def _(group=group):
                 direct_part(group).wait_recv()
 
-        @pl.when(t == 2)
-        def _():
-            for s in range(1, 4):
-                remote(four, four, b_send, b_recv.at[s - 1], other).wait_recv()
-                for i in range(4):
-                    line = part_of(line_column(y + i * y_first - s * (1 - y_first), x + i * (1 - y_first) - s * y_first))
-                    remote(line, line, c_send.at[s], c_recv.at[s], other).start()
-
-        @pl.when(t == 3)
-        def _():
-            for s in range(4):
-                remote(four, four, c_send.at[s], c_recv.at[s], other).wait_recv()
-
-        @pl.when((t >= 3) & (t < 7))
-        def _():
-            def pick(i, inner):
-                wbuf[n_dev + i] = cbuf[plan_ref[4, (t - 3) * GROUP + i]]
-                return inner
-            lax.fori_loop(0, GROUP, pick, 0)
-
-        @pl.when(t == 7)
-        def _():
-            direct_part(3).wait_recv()
-
-        attend(jnp.where(t < 3, t, jnp.where(t < 7, 4, 3)) * GROUP)
+        attend(jnp.where(t < 1, 0, jnp.where(t < 5, 4, t - 4)) * GROUP)
         return carry
 
     lax.fori_loop(0, 8, step, 0)
@@ -392,11 +406,10 @@
 
     lax.fori_loop(0, kv_heads, finish, 0)
     remote(z_three, z_three, z_send, z_recv, other).wait_send()
-    remote(three, three, a_send, a_recv, other).wait_send()
-    twelve = cbuf.at[pl.ds(0, 12 * COMMON)]
-    remote(twelve, twelve, b_send, b_recv.at[0], other).wait_send()
-    for s in range(4):
-        remote(four, four, c_send.at[s], c_recv.at[s], other).wait_send()
+    share(0, 3 * COMMON, a_send, a_recv.at[0], other).wait_send()
+    share(0, 12 * COMMON, b_send, b_recv.at[0], other).wait_send()
+    for i in range(4):
+        share(0, 4 * COMMON, c_send.at[i], c_recv.at[i], other).wait_send()
     for group in range(4):
         direct_part(group).wait_send()
 
@@ -426,7 +439,7 @@
             pltpu.VMEM((kv_heads, 1, q_rows), f32),
             pltpu.VMEM((kv_heads, 1, q_rows), f32)]
         + [pltpu.VMEM((keys, q_tile), f32)] * 4 + [pltpu.VMEM((keys, q_tile), bf16)] * 4 + [pltpu.VMEM((1, q_tile), f32)] * 4
-        + [dma, dma, dma, dma, dma, dma((3,)), dma((4,)), dma((4,)), dma((4,)), dma((4,))],
+        + [dma, dma, dma, dma((3,)), dma, dma((12,)), dma((4,)), dma((4,)), dma((4,)), dma((4,))],
         compiler_params=pltpu.CompilerParams(has_side_effects=True, collective_id=0, vmem_limit_bytes=66_000_000),
         name='fused_attention')(plan, q_grp, k_own, v_own, kv)
     return out.reshape(q_heads, chunk_len, head_dim)

time: 260 us -> 218 us (0.84)
  the two profiles are of different devices: /device:TPU:37 before, /device:TPU:19 now
where the time goes in v4:
time: 218 us
  Pallas kernels  203 us (93%)
  local copies, waits for them, and re-layouts  13.6 us (6%)
    pallas_call x1, Pallas kernels, fused_attention(): pl.pallas_call(fused_kernel, out_shape=jax.ShapeDtypeStruct(q_grp.shape,...  190 us
    pallas_call x1, Pallas kernels, plan_exchange(): pl.pallas_call(plan_kernel, out_shape=jax.ShapeDtypeStruct((8, n_dev), jn...  8.75 us
    pallas_call x1, Pallas kernels, store_chunk(): pl.pallas_call(store_kernel, out_shape=(jax.ShapeDtypeStruct(k_pool.shape...  4.89 us

profile of v4, /device:TPU:19, one launch (start us, length us, event | category | flops | bytes accessed | tf_op | source)
XLA Modules:
  0.0 218.1 jit_solution(6974705599041585362)
XLA Ops:
  0.6 8.8 %plan_exchange.1 = s32[8,128]{1,0:T(8,128)} custom-call(s32[128,256]{1,0:T(8,128)} %tab_ref.1), custom_call_target="tpu_custom_call" | custom-call | tf_op jit(solution)/shard_map/plan_exchange/pallas_call | solution.py:148
  9.4 1.2 slice.15
  11.2 4.9 %store_chunk.1 = (bf16[32,16,8,128]{3,2,1,0:T(8,128)(2,1)}, bf16[32,16,8,128]{3,2,1,0:T(8,128)(2,1)}, bf16[32,2,8,16,128]{4,3,2,1,0:T(8,128)(2,1)}) custom-call(s32[16]{0:T(128)} %bitcast.143, bf16[32,16,8,128]{3,2,1,0:T(8,128)(2,1)} %kp_ref.1, bf16[32,16,8,128]{3,2,1,0:T(8,128)(2,1)} %vp_ref.1, bf16[16,16,8,128]{3,2,1,0:T(8,128)(2,1)} %bitcast.132, ...), custom_call_target="tpu_custom_call" | custom-call | tf_op jit(solution)/shard_map/store_chunk/pallas_call | solution.py:178
  16.1 199.0 %conditional.1 = (bf16[32,256,128]{1,2,0:T(8,128)(2,1)S(1)}) conditional(s32[]{:T(128)} %bitcast.46, (s32[128,256]{1,0:T(8,128)}, bf16[32,16,8,128]{3,2,1,0:T(8,128)(2,1)}, bf16[32,16,8,128]{3,2,1,0:T(8,128)(2,1)}, bf16[1,256,32,128]{3,2,1,0:T(8,128)(2,1)}, bf16[1,256,8,128]{3,2,1,0:T(8,128)(2,1)}, ...), branch_computations={%region_0.11_spmd, %region_11.12_spmd} | conditional | flops 18593110016 | bytes 726269184 | solution.py:454
  16.1 2.4 %copy_bitcast_fusion = (bf16[8,256,128]{2,1,0:T(8,128)(2,1)}, bf16[8,256,128]{2,1,0:T(8,128)(2,1)}) fusion(bf16[1,256,8,128]{3,2,1,0:T(8,128)(2,1)} %get-tuple-element.75, bf16[1,256,8,128]{3,2,1,0:T(8,128)(2,1)} %get-tuple-element.74), kind=kLoop, calls=%fused_computation.5 | loop fusion | bytes 2097152 | tf_op jit(solution)/shard_map/cond/branch_1_fun/transpose | solution.py:421
  18.5 3.8 %copy.58 = bf16[1,256,32,128]{3,1,2,0:T(8,128)(2,1)} copy(bf16[1,256,32,128]{3,2,1,0:T(8,128)(2,1)} %get-tuple-element.73) | data formatting | bytes 4194304 | tf_op jit(solution)/shard_map
  22.2 189.6 %fused_attention.1 = bf16[8,1024,128]{2,1,0:T(8,128)(2,1)} custom-call(s32[8,128]{1,0:T(8,128)} %get-tuple-element.31.plan_ref, bf16[8,1024,128]{2,1,0:T(8,128)(2,1)} %bitcast.130, bf16[8,256,128]{2,1,0:T(8,128)(2,1)} %get-tuple-element.81.kn_ref, bf16[8,256,128]{2,1,0:T(8,128)(2,1)} %get-tuple-element.80.vn_ref, ...), custom_call_target="tpu_custom_call" | custom-call | tf_op jit(solution)/shard_map/cond/branch_1_fun/fused_attention/pallas_call | solution.py:428
  211.8 3.3 %copy.40 = bf16[32,256,128]{1,2,0:T(8,128)(2,1)S(1)} copy(bf16[32,256,128]{2,1,0:T(8,128)(2,1)} %bitcast.129) | data formatting | bytes 4194304 | tf_op jit(solution)/shard_map/cond/branch_1_fun/reshape | solution.py:445
  215.1 3.1 %copy.61 = bf16[32,256,128]{2,0,1:T(8,128)(2,1)} copy(bf16[32,256,128]{1,2,0:T(8,128)(2,1)S(1)} %get-tuple-element.86) | data formatting | bytes 4194304 | tf_op jit(solution)/shard_map/cond | solution.py:454

commit v5 on v4

--- a/solution.py
+++ b/solution.py
@@ -11,6 +11,7 @@
 COMMON = 8
 GROUP = 32
 MESH = pl.DeviceIdType.MESH
+PLACES = (0, 1, 3, 4, 12, 5, 15, 2, 8, 7, 13, 6, 9, 14, 11, 10)
 
 
 def chunk_attention(q_grp, k_pref, v_pref, k_chunk, v_chunk):
@@ -188,12 +189,12 @@
     return z * 32 + y * 8 + x * 2 + c
 
 
-def fused_kernel(plan_ref, q_ref, kn_ref, vn_ref, kv_ref, o_ref,
-                 zbuf, cbuf, sbuf, wbuf, acc_ref, m_ref, l_ref, s0, s1, s2, s3, p0, p1, p2, p3, f0, f1, f2, f3,
+def fused_kernel(plan_ref, q_in, kn_in, vn_in, kv_ref, o_ref,
+                 q_ref, kn_ref, vn_ref, zbuf, cbuf, sbuf, wbuf, acc_ref, m_ref, l_ref, s0, s1, s2, s3, p0, p1, p2, p3, f0, f1, f2, f3,
                  z_send, z_recv, a_send, a_recv, b_send, b_recv, c_send, c_recv, w_send, w_recv):
     n_dev, kv_heads = 128, kn_ref.shape[0]
     heads = 4
-    q_tile = q_ref.shape[1] // heads
+    q_tile = q_ref.shape[1]
     block_len = kv_ref.shape[3]
     scale = math.log2(math.e) * q_ref.shape[2] ** -0.5
     s_bufs, p_bufs, f_bufs = (s0, s1, s2, s3), (p0, p1, p2, p3), (f0, f1, f2, f3)
@@ -205,13 +206,21 @@
 
     def offset_peer(i):
         r = (i * 11) % 32
-        dz = jnp.where(i < 32, 0, i % 3 + 1)
-        return device_at((z + dz * sign) % 4, (y + (r // 8) * sign) % 4, (x + (r // 2) % 4 * sign) % 4, (c + r) % 2)
+        rest = jnp.maximum(i - 32, 0)
+        place = rest // 6
+        in_plane = jnp.int32(PLACES[-1])
+        for n in range(len(PLACES) - 2, -1, -1):
+            in_plane = jnp.where(place == n, PLACES[n], in_plane)
+        near = i < 32
+        in_plane = jnp.where(near, r // 2, in_plane)
+        dz = jnp.where(near, 0, rest % 3 + 1)
+        dc = jnp.where(near, r, rest % 6 // 3)
+        return device_at((z + dz * sign) % 4, (y + in_plane // 4 * sign) % 4, (x + in_plane % 4 * sign) % 4, (c + dc) % 2)
 
     barrier = pltpu.get_barrier_semaphore()
 
     def greet(i, carry):
-        pl.semaphore_signal(barrier, inc=1, device_id=(offset_peer(i),), device_id_type=MESH)
+        pl.semaphore_signal(barrier, inc=1, device_id=((me + i) % n_dev,), device_id_type=MESH)
         return carry
 
     lax.fori_loop(1, n_dev, greet, 0)
@@ -251,13 +260,22 @@
 
     send_direct(0)
 
+    def heads_first(t, carry):
+        rows = pl.ds(t * block_len, block_len)
+        q_ref[:, rows, :] = jnp.swapaxes(q_in[rows], 0, 1)
+        kn_ref[:, rows, :] = jnp.swapaxes(kn_in[rows], 0, 1)
+        vn_ref[:, rows, :] = jnp.swapaxes(vn_in[rows], 0, 1)
+        return carry
+
+    lax.fori_loop(0, q_tile // block_len, heads_first, 0)
+
     row = lax.broadcasted_iota(jnp.int32, (kn_ref.shape[1], q_tile), 0)
     token = lax.broadcasted_iota(jnp.int32, (kn_ref.shape[1], q_tile), 1)
 
     def own_head(g, carry):
         for h in range(heads):
             cols = pl.ds(h * q_tile, q_tile)
-            s = lax.dot_general(kn_ref[g], q_ref[g, cols, :], NT, preferred_element_type=jnp.float32)
+            s = lax.dot_general(kn_ref[g], q_ref[g * heads + h], NT, preferred_element_type=jnp.float32)
             s = jnp.where(row <= token, s, -jnp.inf)
             top = jnp.max(s, axis=0, keepdims=True)
             e = jnp.exp2((s - top) * scale)
@@ -275,7 +293,7 @@
             return wbuf[pl.ds(start, GROUP), which, g].reshape(GROUP * block_len, kv_ref.shape[4])
 
         def score(g, h):
-            s_bufs[h][...] = lax.dot_general(rows_of(0, g), q_ref[g, pl.ds(h * q_tile, q_tile), :], NT, preferred_element_type=jnp.float32)
+            s_bufs[h][...] = lax.dot_general(rows_of(0, g), q_ref[g * heads + h], NT, preferred_element_type=jnp.float32)
 
         def weigh(g, h):
             cols = pl.ds(h * q_tile, q_tile)
@@ -349,6 +367,7 @@
     share(line_at(0, 0), COMMON, a_send, a_recv.at[0], next_a).start()
     share(line_at(0, 0), COMMON, a_send, a_recv.at[1], prev_a).start()
     to_second(0, 0)
+    send_direct(1)
     arrived(COMMON, a_send, a_recv.at[0])
     share(line_at(3, 0), half, a_send, a_recv.at[2], next_a).start()
     to_second(1, 3)
@@ -364,7 +383,7 @@
         arrived(COMMON, b_send, b_recv.at[3 * i + 1])
         share(line_at(first, 1) + half, half, b_send, b_recv.at[3 * i + 2], prev_b).start()
         share(line_at(first, 1), COMMON, c_send.at[2], c_recv.at[2], other).start()
-    for group in range(1, 4):
+    for group in range(2, 4):
         send_direct(group)
     for i, first in enumerate(order):
         arrived(COMMON, b_send, b_recv.at[3 * i + 2])
@@ -401,10 +420,17 @@
         for h in range(heads):
             cols = pl.ds(h * q_tile, q_tile)
             out = acc_ref[g, :, cols] / l_ref[g, :, cols]
-            o_ref[g, cols, :] = out.T.astype(jnp.bfloat16)
+            q_ref[g * heads + h] = out.T.astype(jnp.bfloat16)
         return carry
 
     lax.fori_loop(0, kv_heads, finish, 0)
+
+    def tokens_first(t, carry):
+        rows = pl.ds(t * block_len, block_len)
+        o_ref[rows] = jnp.swapaxes(q_ref[:, rows, :], 0, 1)
+        return carry
+
+    lax.fori_loop(0, q_tile // block_len, tokens_first, 0)
     remote(z_three, z_three, z_send, z_recv, other).wait_send()
     share(0, 3 * COMMON, a_send, a_recv.at[0], other).wait_send()
     share(0, 12 * COMMON, b_send, b_recv.at[0], other).wait_send()
@@ -417,20 +443,21 @@
 def fused_attention(queries, k_new, v_new, kv, plan):
     _, chunk_len, q_heads, head_dim = queries.shape
     kv_heads = k_new.shape[2]
-    q_grp = queries[0].transpose(1, 0, 2).reshape(kv_heads, -1, head_dim)
-    k_own, v_own = k_new[0].transpose(1, 0, 2), v_new[0].transpose(1, 0, 2)
     block = kv.shape[1:]
-    q_rows, q_tile = q_grp.shape[1], q_grp.shape[1] // 4
+    q_rows, q_tile = chunk_len * q_heads // kv_heads, chunk_len
     keys = GROUP * block[2]
     bf16, f32 = jnp.bfloat16, jnp.float32
     smem, vmem = pl.BlockSpec(memory_space=pltpu.SMEM), pl.BlockSpec(memory_space=pltpu.VMEM)
     dma = pltpu.SemaphoreType.DMA
     out = pl.pallas_call(
         fused_kernel,
-        out_shape=jax.ShapeDtypeStruct(q_grp.shape, bf16),
+        out_shape=jax.ShapeDtypeStruct(queries.shape[1:], bf16),
         in_specs=[smem] + [vmem] * 4,
         out_specs=vmem,
         scratch_shapes=[
+            pltpu.VMEM((q_heads, chunk_len, head_dim), bf16),
+            pltpu.VMEM((kv_heads, chunk_len, head_dim), bf16),
+            pltpu.VMEM((kv_heads, chunk_len, head_dim), bf16),
             pltpu.VMEM((4 * COMMON,) + block, bf16),
             pltpu.VMEM((32 * COMMON,) + block, bf16),
             pltpu.VMEM((128,) + block, bf16),
@@ -441,8 +468,8 @@
         + [pltpu.VMEM((keys, q_tile), f32)] * 4 + [pltpu.VMEM((keys, q_tile), bf16)] * 4 + [pltpu.VMEM((1, q_tile), f32)] * 4
         + [dma, dma, dma, dma((3,)), dma, dma((12,)), dma((4,)), dma((4,)), dma((4,)), dma((4,))],
         compiler_params=pltpu.CompilerParams(has_side_effects=True, collective_id=0, vmem_limit_bytes=66_000_000),
-        name='fused_attention')(plan, q_grp, k_own, v_own, kv)
-    return out.reshape(q_heads, chunk_len, head_dim)
+        name='fused_attention')(plan, queries[0], k_new[0], v_new[0], kv)
+    return out
 
 
 def solution(mesh):
@@ -451,11 +478,11 @@
     def local_step(queries, k_new, v_new, k_pool, v_pool, block_table, write_ids):
         plan = plan_exchange(block_table)
         k_pool_out, v_pool_out, kv = store_chunk(k_pool, v_pool, k_new, v_new, write_ids)
-        by_head = lax.cond(
+        attn_out = lax.cond(
             plan[0, 0] == 0,
             lambda: fused_attention(queries, k_new, v_new, kv, plan),
-            lambda: general_attention(n_dev, queries, k_new, v_new, k_pool, v_pool, block_table)[0].transpose(1, 0, 2))
-        return by_head.transpose(1, 0, 2)[None], k_pool_out, v_pool_out
+            lambda: general_attention(n_dev, queries, k_new, v_new, k_pool, v_pool, block_table)[0])
+        return attn_out[None], k_pool_out, v_pool_out
 
     row_spec = P('pool')
     return jax.shard_map(local_step, mesh=mesh, in_specs=(row_spec, row_spec, row_spec, row_spec, row_spec, P(), row_spec), out_specs=(row_spec, row_spec, row_spec), check_vma=False)

time: 218 us -> 211 us (0.968)
  the two profiles are of different devices: /device:TPU:19 before, /device:TPU:46 now
where the time goes in v5:
time: 211 us
  Pallas kernels  205 us (97%)
  local copies, waits for them, and re-layouts  4.46 us (2%)
    pallas_call x1, Pallas kernels, fused_attention(): pl.pallas_call(fused_kernel, out_shape=jax.ShapeDtypeStruct(queries.shape...  191 us
    pallas_call x1, Pallas kernels, plan_exchange(): pl.pallas_call(plan_kernel, out_shape=jax.ShapeDtypeStruct((8, n_dev), jn...  8.75 us
    pallas_call x1, Pallas kernels, store_chunk(): pl.pallas_call(store_kernel, out_shape=(jax.ShapeDtypeStruct(k_pool.shape...  4.89 us

profile of v5, /device:TPU:46, one launch (start us, length us, event | category | flops | bytes accessed | tf_op | source)
XLA Modules:
  0.0 210.6 jit_solution(4656351469583119710)
XLA Ops:
  0.6 8.8 %plan_exchange.1 = s32[8,128]{1,0:T(8,128)} custom-call(s32[128,256]{1,0:T(8,128)} %tab_ref.1), custom_call_target="tpu_custom_call" | custom-call | tf_op jit(solution)/shard_map/plan_exchange/pallas_call | solution.py:149
  9.4 1.2 slice.15
  11.2 4.9 %store_chunk.1 = (bf16[32,16,8,128]{3,2,1,0:T(8,128)(2,1)}, bf16[32,16,8,128]{3,2,1,0:T(8,128)(2,1)}, bf16[32,2,8,16,128]{4,3,2,1,0:T(8,128)(2,1)}) custom-call(s32[16]{0:T(128)} %bitcast.128, bf16[32,16,8,128]{3,2,1,0:T(8,128)(2,1)} %kp_ref.1, bf16[32,16,8,128]{3,2,1,0:T(8,128)(2,1)} %vp_ref.1, bf16[16,16,8,128]{3,2,1,0:T(8,128)(2,1)} %bitcast.116, ...), custom_call_target="tpu_custom_call" | custom-call | tf_op jit(solution)/shard_map/store_chunk/pallas_call | solution.py:179
  16.1 191.2 %conditional.1 = (bf16[1,256,32,128]{3,2,1,0:T(8,128)(2,1)}) conditional(s32[]{:T(128)} %bitcast.41, (s32[128,256]{1,0:T(8,128)}, bf16[32,16,8,128]{3,2,1,0:T(8,128)(2,1)}, bf16[32,16,8,128]{3,2,1,0:T(8,128)(2,1)}, bf16[1,256,32,128]{3,2,1,0:T(8,128)(2,1)}, bf16[1,256,8,128]{3,2,1,0:T(8,128)(2,1)}, ...), branch_computations={%region_0.11_spmd, %region_11.12_spmd} | conditional | flops 18593110016 | bytes 730463488 | solution.py:481
  16.1 191.2 %fused_attention.1 = bf16[256,32,128]{2,1,0:T(8,128)(2,1)} custom-call(s32[8,128]{1,0:T(8,128)} %get-tuple-element.32.plan_ref, bf16[256,32,128]{2,1,0:T(8,128)(2,1)} %bitcast.114, bf16[256,8,128]{2,1,0:T(8,128)(2,1)} %bitcast.117, bf16[256,8,128]{2,1,0:T(8,128)(2,1)} %bitcast.120, bf16[32,2,8,16,128]{4,3,2,1,0:T(8,128)(2,1)} %get-tuple-element.36.kv_ref), custom_call_target="tpu_custom_call" | custom-call | tf_op jit(solution)/shard_map/cond/branch_1_fun/fused_attention/pallas_call | solution.py:452
  207.3 3.3 %copy.91 = bf16[1,256,32,128]{3,2,1,0:T(8,128)(2,1)} copy(bf16[1,256,32,128]{3,2,1,0:T(8,128)(2,1)} %get-tuple-element.85) | data formatting | bytes 4194304

commit v6 on v5

--- a/solution.py
+++ b/solution.py
@@ -64,7 +64,7 @@
 TN = (((0,), (0,)), ((), ()))
 
 
-def plan_kernel(tab_ref, plan_ref, named_ref, least_ref):
+def plan_kernel(tab_ref, plan_ref, flag_ref, named_ref, least_ref):
     f32, bf16, i32 = jnp.float32, jnp.bfloat16, jnp.int32
     n_dev, n_pref = tab_ref.shape
     per_dev, n_col = 32, n_dev // 4
@@ -138,6 +138,7 @@
     for l in range(per_dev):
         pick = pick + jnp.where(place[:, l:l + 1] == j_lane, slot_t[:, l:l + 1], 0.0)
     pick = jnp.sum(pick, axis=0, keepdims=True)
+    flag_ref[0] = misfit.astype(i32)
     plan_ref[...] = jnp.zeros(plan_ref.shape, i32)
     for i, value in enumerate((misfit + jnp.zeros((1, n_dev), f32), direct, own, col, pick)):
         plan_ref[i:i + 1, :] = value.astype(i32)
@@ -148,9 +149,9 @@
     vmem = pl.BlockSpec(memory_space=pltpu.VMEM)
     return pl.pallas_call(
         plan_kernel,
-        out_shape=jax.ShapeDtypeStruct((8, n_dev), jnp.int32),
+        out_shape=(jax.ShapeDtypeStruct((8, n_dev), jnp.int32), jax.ShapeDtypeStruct((1,), jnp.int32)),
         in_specs=[vmem],
-        out_specs=vmem,
+        out_specs=(vmem, pl.BlockSpec(memory_space=pltpu.SMEM)),
         scratch_shapes=[pltpu.VMEM((n_dev, 32, n_dev), jnp.float32), pltpu.VMEM((n_dev, n_dev), jnp.float32)],
         name='plan_exchange')(block_table)
 
@@ -217,6 +218,8 @@
         dc = jnp.where(near, r, rest % 6 // 3)
         return device_at((z + dz * sign) % 4, (y + in_plane // 4 * sign) % 4, (x + in_plane % 4 * sign) % 4, (c + dc) % 2)
 
+    groups = n_dev // GROUP
+    near_groups = groups // 4
     barrier = pltpu.get_barrier_semaphore()
 
     def greet(i, carry):
@@ -235,7 +238,8 @@
     def fill_group(group):
         lax.fori_loop(max(1, group * GROUP), (group + 1) * GROUP, fill, 0)
 
-    fill_group(0)
+    for group in range(near_groups):
+        fill_group(group)
     wbuf[0] = kv_ref[plan_ref[1, me]]
     pl.semaphore_wait(barrier, n_dev - 1)
 
@@ -258,7 +262,8 @@
         part = wbuf.at[pl.ds(0, size)]
         return remote(part, part, w_send.at[group], w_recv.at[group], other)
 
-    send_direct(0)
+    for group in range(near_groups):
+        send_direct(group)
 
     def heads_first(t, carry):
         rows = pl.ds(t * block_len, block_len)
@@ -285,7 +290,7 @@
         return carry
 
     lax.fori_loop(0, kv_heads, own_head, 0)
-    for group in range(1, 4):
+    for group in range(near_groups, groups):
         fill_group(group)
 
     def attend(start):
@@ -367,7 +372,8 @@
     share(line_at(0, 0), COMMON, a_send, a_recv.at[0], next_a).start()
     share(line_at(0, 0), COMMON, a_send, a_recv.at[1], prev_a).start()
     to_second(0, 0)
-    send_direct(1)
+    for group in range(near_groups, 2 * near_groups):
+        send_direct(group)
     arrived(COMMON, a_send, a_recv.at[0])
     share(line_at(3, 0), half, a_send, a_recv.at[2], next_a).start()
     to_second(1, 3)
@@ -383,38 +389,36 @@
         arrived(COMMON, b_send, b_recv.at[3 * i + 1])
         share(line_at(first, 1) + half, half, b_send, b_recv.at[3 * i + 2], prev_b).start()
         share(line_at(first, 1), COMMON, c_send.at[2], c_recv.at[2], other).start()
-    for group in range(2, 4):
+    for group in range(2 * near_groups, groups):
         send_direct(group)
     for i, first in enumerate(order):
         arrived(COMMON, b_send, b_recv.at[3 * i + 2])
         share(line_at(first, 2), COMMON, c_send.at[3], c_recv.at[3], other).start()
 
+    last_common = near_groups + groups
+
     def step(t, carry):
-        @pl.when(t == 0)
-        def _():
-            direct_part(0).wait_recv()
-
-        @pl.when(t == 1)
+        for group in range(groups):
+            @pl.when(t == (group if group < near_groups else group + groups))
+            def _(group=group):
+                direct_part(group).wait_recv()
+
+        @pl.when(t == near_groups)
         def _():
             for i in range(4):
                 arrived(4 * COMMON, c_send.at[i], c_recv.at[i])
 
-        @pl.when((t >= 1) & (t < 5))
+        @pl.when((t >= near_groups) & (t < last_common))
         def _():
             def pick(i, inner):
-                wbuf[n_dev + i] = cbuf[plan_ref[4, (t - 1) * GROUP + i]]
+                wbuf[n_dev + i] = cbuf[plan_ref[4, (t - near_groups) * GROUP + i]]
                 return inner
             lax.fori_loop(0, GROUP, pick, 0)
 
-        for group in range(1, 4):
-            @pl.when(t == group + 4)
-            def _(group=group):
-                direct_part(group).wait_recv()
-
-        attend(jnp.where(t < 1, 0, jnp.where(t < 5, 4, t - 4)) * GROUP)
-        return carry
-
-    lax.fori_loop(0, 8, step, 0)
+        attend(jnp.where(t < near_groups, t, jnp.where(t < last_common, groups, t - groups)) * GROUP)
+        return carry
+
+    lax.fori_loop(0, 2 * groups, step, 0)
 
     def finish(g, carry):
         for h in range(heads):
@@ -436,7 +440,7 @@
     share(0, 12 * COMMON, b_send, b_recv.at[0], other).wait_send()
     for i in range(4):
         share(0, 4 * COMMON, c_send.at[i], c_recv.at[i], other).wait_send()
-    for group in range(4):
+    for group in range(groups):
         direct_part(group).wait_send()
 
 
@@ -466,7 +470,7 @@
             pltpu.VMEM((kv_heads, 1, q_rows), f32),
             pltpu.VMEM((kv_heads, 1, q_rows), f32)]
         + [pltpu.VMEM((keys, q_tile), f32)] * 4 + [pltpu.VMEM((keys, q_tile), bf16)] * 4 + [pltpu.VMEM((1, q_tile), f32)] * 4
-        + [dma, dma, dma, dma((3,)), dma, dma((12,)), dma((4,)), dma((4,)), dma((4,)), dma((4,))],
+        + [dma, dma, dma, dma((3,)), dma, dma((12,)), dma((4,)), dma((4,)), dma((128 // GROUP,)), dma((128 // GROUP,))],
         compiler_params=pltpu.CompilerParams(has_side_effects=True, collective_id=0, vmem_limit_bytes=66_000_000),
         name='fused_attention')(plan, queries[0], k_new[0], v_new[0], kv)
     return out
@@ -476,10 +480,10 @@
     n_dev = mesh.shape['pool']
 
     def local_step(queries, k_new, v_new, k_pool, v_pool, block_table, write_ids):
-        plan = plan_exchange(block_table)
+        plan, misfit = plan_exchange(block_table)
         k_pool_out, v_pool_out, kv = store_chunk(k_pool, v_pool, k_new, v_new, write_ids)
         attn_out = lax.cond(
-            plan[0, 0] == 0,
+            misfit[0] == 0,
             lambda: fused_attention(queries, k_new, v_new, kv, plan),
             lambda: general_attention(n_dev, queries, k_new, v_new, k_pool, v_pool, block_table)[0])
         return attn_out[None], k_pool_out, v_pool_out

time: 211 us -> 209 us (level)
  no operation moved by 1% of the time
where the time goes in v6:
time: 209 us
  Pallas kernels  204 us (98%)
  local copies, waits for them, and re-layouts  3.27 us (2%)
    pallas_call x1, Pallas kernels, fused_attention(): pl.pallas_call(fused_kernel, out_shape=jax.ShapeDtypeStruct(queries.shape...  191 us
    pallas_call x1, Pallas kernels, plan_exchange(): pl.pallas_call(plan_kernel, out_shape=(jax.ShapeDtypeStruct((8, n_dev), j...  8.17 us
    pallas_call x1, Pallas kernels, store_chunk(): pl.pallas_call(store_kernel, out_shape=(jax.ShapeDtypeStruct(k_pool.shape...  4.89 us

profile of v6, /device:TPU:46, one launch (start us, length us, event | category | flops | bytes accessed | tf_op | source)
XLA Modules:
  0.0 208.8 jit_solution(17710947173839114549)
XLA Ops:
  0.6 8.2 %plan_exchange.1 = (s32[8,128]{1,0:T(8,128)S(1)}, s32[1]{0:T(128)}) custom-call(s32[128,256]{1,0:T(8,128)} %tab_ref.1), custom_call_target="tpu_custom_call" | custom-call | tf_op jit(solution)/shard_map/plan_exchange/pallas_call | solution.py:150
  9.5 4.9 %store_chunk.1 = (bf16[32,16,8,128]{3,2,1,0:T(8,128)(2,1)}, bf16[32,16,8,128]{3,2,1,0:T(8,128)(2,1)}, bf16[32,2,8,16,128]{4,3,2,1,0:T(8,128)(2,1)}) custom-call(s32[16]{0:T(128)} %bitcast.128, bf16[32,16,8,128]{3,2,1,0:T(8,128)(2,1)} %kp_ref.1, bf16[32,16,8,128]{3,2,1,0:T(8,128)(2,1)} %vp_ref.1, bf16[16,16,8,128]{3,2,1,0:T(8,128)(2,1)} %bitcast.116, ...), custom_call_target="tpu_custom_call" | custom-call | tf_op jit(solution)/shard_map/store_chunk/pallas_call | solution.py:180
  14.3 191.2 %conditional.1 = (bf16[1,256,32,128]{3,2,1,0:T(8,128)(2,1)}) conditional(s32[]{:T(128)} %bitcast.41, (s32[128,256]{1,0:T(8,128)}, bf16[32,16,8,128]{3,2,1,0:T(8,128)(2,1)}, bf16[32,16,8,128]{3,2,1,0:T(8,128)(2,1)}, bf16[1,256,32,128]{3,2,1,0:T(8,128)(2,1)}, bf16[1,256,8,128]{3,2,1,0:T(8,128)(2,1)}, ...), branch_computations={%region_0.11_spmd, %region_11.12_spmd} | conditional | flops 18593110016 | bytes 730463488 | solution.py:485
  14.3 191.2 %fused_attention.1 = bf16[256,32,128]{2,1,0:T(8,128)(2,1)} custom-call(s32[8,128]{1,0:T(8,128)S(1)} %get-tuple-element.32.plan_ref, bf16[256,32,128]{2,1,0:T(8,128)(2,1)} %bitcast.114, bf16[256,8,128]{2,1,0:T(8,128)(2,1)} %bitcast.117, bf16[256,8,128]{2,1,0:T(8,128)(2,1)} %bitcast.120, bf16[32,2,8,16,128]{4,3,2,1,0:T(8,128)(2,1)} %get-tuple-element.36.kv_ref), custom_call_target="tpu_custom_call" | custom-call | tf_op jit(solution)/shard_map/cond/branch_1_fun/fused_attention/pallas_call | solution.py:456
  205.5 3.3 %copy.91 = bf16[1,256,32,128]{3,2,1,0:T(8,128)(2,1)} copy(bf16[1,256,32,128]{3,2,1,0:T(8,128)(2,1)} %get-tuple-element.89) | data formatting | bytes 4194304
